TPU v7x, 128 devices: a whole 4x4x4 slice. The times are simulated.
128 devices in a mesh: gx: 8 (over z, core), gy: 16 (over x, y).
Axes of the slice: x: 4, y: 4, z: 4, core: 2. Of those that a mesh axis runs over, the one named last changes fastest.
Arguments:
- prolong: bfloat16 [8192, 24, 128], P(('gx', 'gy')), may hold values from -0.5 to 0.5
- stiffness: bfloat16 [16384, 4, 128, 128], P(('gx', 'gy')), may hold values from -6 to 6
- request: int32 [16384], P(('gx', 'gy')), may hold values from 0 to 63, as said below
- col_slot: int32 [16384, 4], P(('gx', 'gy')), may hold values from 0 to 127
- col_pos: int32 [16384, 4], P(('gx', 'gy')), may hold values from 0 to 15, as said below
- coarse_owner: int32 [8192, 1], P(('gx', 'gy')), may hold values from 0 to 127; in each aligned block of 64 rows (0 to 63, 64 to 127, ...) no two rows name the same one
Outputs:
- coarse: float32 [16384, 24, 384], P(('gx', 'gy'))
Inputs may be any that keep to these rules, and one draw needn't show every extreme that they name: `request`: on each device, entries k * 1 to (k + 1) * 1 - 1 name distinct aggregates of device k, as local indices there. `col_pos`: the 4 entries of one block row are distinct. `coarse_owner`: among one device's 64 aggregates at most 1 share a coarse owner, and on some devices 1 do.
All inputs are finite; a program needn't handle non-finite values.
Results may differ from a plain program's by a relative error of at most 0.0003.
Values may be sent and summed in bfloat16 or wider, within the bound.
No kernel may reach another device: no remote copies, remote signals or barrier semaphores. Data moves between devices by JAX's collectives and lax.ppermute only.
A program may use at most 128 MiB of HBM per device.

v0:
```python
import jax
import jax.numpy as jnp
from jax import lax
from jax.sharding import PartitionSpec as P

MAXNB = 16


HIGH = lax.Precision.HIGHEST


def side_by_side(arrays, axis, split_dim, concat_dim, along):
    columns = [a.reshape(*a.shape[:along], -1) for a in arrays]
    both = jnp.concatenate(columns, axis=along)
    result, at, done = (
        lax.all_to_all(both, axis, split_axis=split_dim, concat_axis=concat_dim, tiled=True),
        0,
        [],
    )
    for a, column in zip(arrays, columns):
        slab = result[..., at : at + column.shape[along]]
        done.append(slab.reshape(*slab.shape[:along], *a.shape[along:]))
        at += column.shape[along]
    return tuple(done)


def placed(partial_value, column_hot):
    spread = jnp.einsum("tqce,tqn->tcne", partial_value, column_hot, precision=HIGH)
    return spread.reshape(
        partial_value.shape[0], partial_value.shape[2], column_hot.shape[2] * partial_value.shape[3]
    )


def per_device(prolong, stiffness, request, col_slot, col_pos, coarse_owner):
    devices = lax.axis_size(("gx", "gy"))
    own_aggs = prolong.shape[0]
    columns = MAXNB
    requested = lax.all_to_all(request, ("gx", "gy"), split_axis=0, concat_axis=0, tiled=True)
    fetched = lax.all_to_all(
        prolong[requested], ("gx", "gy"), split_axis=0, concat_axis=0, tiled=True
    )
    col_rows = fetched[col_slot]
    applied = jnp.einsum("tqij,tqej->tqei", stiffness, col_rows, preferred_element_type=jnp.float32)
    partial_value = jnp.einsum(
        "tci,tqei->tqce", fetched.astype(jnp.float32), applied, precision=HIGH
    )
    blocks_in, where_in = side_by_side(
        (partial_value, col_pos.astype(jnp.float32)), ("gx", "gy"), 0, 0, 2
    )
    hot_in = (where_in[:, :, None] == jnp.arange(columns, dtype=jnp.float32)[None, None, :]).astype(
        jnp.float32
    )
    rows_in = placed(blocks_in, hot_in)
    owner_hot = (requested[None, :] == jnp.arange(own_aggs, dtype=jnp.int32)[:, None]).astype(
        jnp.float32
    )
    fine_rows = jnp.einsum("at,tcw->acw", owner_hot, rows_in, precision=HIGH)
    owners = coarse_owner[:, 0]
    peer_ids = jnp.arange(devices, dtype=jnp.int32)
    owner_one = (owners[:, None] == peer_ids[None, :]).astype(jnp.int32)
    before = jnp.cumsum(owner_one, axis=0) - owner_one
    row_rank = jnp.sum(before * owner_one, axis=1)
    send_max = (2 * own_aggs + devices - 1) // devices
    place_hot = (owners[None, None, :] == peer_ids[:, None, None]) & (
        row_rank[None, None, :] == jnp.arange(send_max, dtype=jnp.int32)[None, :, None]
    )
    outgoing = jnp.einsum("esa,acw->escw", place_hot.astype(jnp.float32), fine_rows, precision=HIGH)
    arrived = lax.all_to_all(outgoing, ("gx", "gy"), split_axis=0, concat_axis=0, tiled=True)
    return arrived.reshape((devices * send_max,) + fine_rows.shape[1:])


def solution(mesh):
    placed = (
        P(("gx", "gy"), None, None),
        P(("gx", "gy"), None, None, None),
        P(("gx", "gy")),
        P(("gx", "gy"), None),
        P(("gx", "gy"), None),
        P(("gx", "gy"), None),
    )
    return jax.shard_map(
        per_device,
        mesh=mesh,
        in_specs=placed,
        out_specs=P(("gx", "gy"), None, None),
        check_vma=False,
    )
```

profile of v0, /device:TPU:1, one launch (start us, length us, event | category | flops | bytes accessed | tf_op | source)
XLA Modules:
  0.0 215.7 jit_solution(2421565605549395762)
XLA Ops:
  0.0 0.0 copy-start
  0.0 0.8 copy.24
  0.8 20.9 %all_to_all.27 = s32[128,1,1]{2,1,0:T(1,128)S(1)} all-to-all(s32[128,1,1]{2,1,0:T(1,128)S(1)} %copy.24), channel_id=1, replica_groups=mesh['gx'=8,'gy'=16] {'gx','gy'}, dimensions={0} | all-to-all | bytes 1024 | tf_op jit(solution)/shard_map/all_to_all | solution.py:38
  21.7 2.3 %reduce = s32[128]{0:T(128)S(1)} reduce(s32[128,1,1]{2,1,0:T(1,128)S(1)} %all_to_all.27, s32[]{:T(128)} %constant.3.clone.1), dimensions={1,2}, to_apply=%all_to_all.18.reduce_sub_computation | reduce | bytes 1028 | tf_op jit(solution)/shard_map/all_to_all | solution.py:38
  24.1 0.0 copy-done
  24.1 1.6 gather_fusion
  25.7 4.5 %all-to-all-start.1 = ((bf16[128,24,128]{2,1,0:T(8,128)(2,1)}), bf16[128,24,128]{2,1,0:T(8,128)(2,1)S(1)}, u32[]{:S(2)}, u32[]{:S(2)}) async-start(bf16[128,24,128]{2,1,0:T(8,128)(2,1)} %gather_fusion), calls=%async_computation.1 | async-start | bytes 1572864 | tf_op jit(solution)/shard_map/all_to_all | solution.py:39
  30.2 0.7 compare_select_fusion
  30.9 0.1 copy.25
  31.0 0.1 reshape.92
  31.1 0.7 convert_element_type.5
  31.8 14.5 %all-to-all-done.1 = bf16[128,24,128]{2,1,0:T(8,128)(2,1)S(1)} async-done(((bf16[128,24,128]{2,1,0:T(8,128)(2,1)}), bf16[128,24,128]{2,1,0:T(8,128)(2,1)S(1)}, u32[]{:S(2)}, u32[]{:S(2)}) %all-to-all-start.1) | async-done | bytes 786464 | tf_op jit(solution)/shard_map/all_to_all | solution.py:39
  46.2 3.2 %gather_fusion.1 = bf16[512,24,128]{2,1,0:T(8,128)(2,1)} fusion(bf16[128,24,128]{2,1,0:T(8,128)(2,1)S(1)} %all-to-all-done.1, s32[1024]{0:T(1024)S(1)} %pad_clamp_fusion), kind=kCustom, calls=%fused_computation.1 | custom fusion | bytes 6293504 | tf_op jit(solution)/shard_map/gather | solution.py:42
  49.4 12.8 %fusion.15 = f32[128,4,24,128]{3,2,1,0:T(8,128)S(1)} fusion(bf16[128,4,24,128]{3,2,1,0:T(8,128)(2,1)} %bitcast.42, bf16[128,4,128,128]{3,2,1,0:T(8,128)(2,1)} %param.7), kind=kOutput, calls=%fused_computation.28 | convolution fusion | flops 402653184 | bytes 26214400 | tf_op jit(solution)/shard_map/tqij,tqej->tqei/dot_general | solution.py:43
  62.2 4.8 %convolution_bitcast_fusion.1 = f32[128,4,24,24]{2,3,1,0:T(8,128)} fusion(f32[128,4,24,128]{3,2,1,0:T(8,128)S(1)} %fusion.15, bf16[128,24,128]{2,1,0:T(8,128)(2,1)S(1)} %all-to-all-done.1), kind=kOutput, calls=%fused_computation.3 | convolution fusion | flops 452984832 | bytes 8257536 | tf_op jit(solution)/shard_map/tci,tqei->tqce/dot_general | solution.py:44
  67.0 5.5 %copy.26 = f32[128,4,24,24]{0,3,2,1:T(8,128)S(1)} copy(f32[128,4,24,24]{2,3,1,0:T(8,128)} %convolution_bitcast_fusion.1) | data formatting | bytes 2359296 | tf_op jit(solution)/shard_map/tci,tqei->tqce/transpose | solution.py:44
  72.4 0.0 copy-start.2
  72.4 0.1 pad_maximum_fusion
  72.5 1.5 copy.27
  74.0 4.8 %all-to-all-start.2 = ((f32[128,4,577]{2,1,0:T(4,128)}), f32[128,4,577]{2,1,0:T(4,128)S(1)}, u32[]{:S(2)}, u32[]{:S(2)}) async-start(f32[128,4,577]{2,1,0:T(4,128)} %copy.27), calls=%async_computation.2 | async-start | bytes 2621440 | tf_op jit(solution)/shard_map/all_to_all | solution.py:16
  78.9 0.0 copy-done.2
  78.9 0.1 fusion.4
  78.9 0.1 reduce_window_sum.11
  79.0 0.2 select_reduce_fusion
  79.2 21.1 %all-to-all-done.2 = f32[128,4,577]{2,1,0:T(4,128)S(1)} async-done(((f32[128,4,577]{2,1,0:T(4,128)}), f32[128,4,577]{2,1,0:T(4,128)S(1)}, u32[]{:S(2)}, u32[]{:S(2)}) %all-to-all-start.2) | async-done | bytes 1181728 | tf_op jit(solution)/shard_map/all_to_all | solution.py:16
  100.3 0.9 copy.38
  101.2 4.6 %copy.31 = f32[128,4,24,24]{3,1,2,0:T(4,128)} copy(f32[128,4,24,24]{0,3,2,1:T(8,128)S(1)} %bitcast.47) | data formatting | bytes 2359296 | tf_op jit(solution)/shard_map/reshape | solution.py:22
  105.8 0.2 slice.12
  106.0 0.1 copy.28
  106.1 0.1 copy.29
  106.3 19.0 %convolution_bitcast_fusion = f32[128,24,16,24]{3,2,1,0:T(8,128)} fusion(f32[128,4,24,24]{3,1,2,0:T(4,128)} %copy.31, f32[128,4]{1,0:T(8,128)S(1)} %copy.29), kind=kOutput, calls=%fused_computation.2 | convolution fusion | flops 56631296 | bytes 5900288 | tf_op jit(solution)/shard_map/tqce,tqn->tcne/dot_general | solution.py:28
  125.3 15.4 %copy.32 = f32[128,24,16,24]{0,3,2,1:T(8,128)} copy(f32[128,24,16,24]{3,2,1,0:T(8,128)} %convolution_bitcast_fusion) | data formatting | bytes 9437184 | tf_op jit(solution)/shard_map/tqce,tqn->tcne/transpose | solution.py:28
  140.7 5.2 %fusion.9 = f32[64,24,384]{2,0,1:T(8,128)S(1)} fusion(f32[128,24,384]{0,2,1:T(8,128)} %bitcast.43, s32[128]{0:T(128)S(1)} %reduce), kind=kOutput, calls=%fused_computation.18 | convolution fusion | flops 905977856 | bytes 7078400 | tf_op jit(solution)/shard_map/at,tcw->acw/dot_general | solution.py:57
  145.9 2.1 convolution_bitcast_fusion.2
  148.1 2.7 %copy.34 = f32[128,1,24,384]{3,2,1,0:T(8,128)S(1)} copy(f32[128,1,24,384]{3,0,2,1:T(8,128)S(1)} %convolution_bitcast_fusion.2) | data formatting | bytes 9437184 | tf_op jit(solution)/shard_map/esa,acw->escw/dot_general | solution.py:67
  150.8 62.7 %all_to_all.28 = f32[128,1,24,384]{3,2,1,0:T(8,128)S(1)} all-to-all(f32[128,1,24,384]{3,2,1,0:T(8,128)S(1)} %copy.34), channel_id=1, replica_groups=mesh['gx'=8,'gy'=16] {'gx','gy'}, dimensions={0} | all-to-all | bytes 9437184 | tf_op jit(solution)/shard_map/all_to_all | solution.py:68
  213.5 0.0 copy-start.1
  213.5 2.2 %copy.40 = f32[128,24,384]{2,1,0:T(8,128)} copy(f32[128,24,384]{2,1,0:T(8,128)S(1)} %bitcast.44) | data formatting | bytes 9437184
  215.7 0.0 copy-done.1
  (4 shorter events, 0.0 us)
Async XLA Ops:
  0.0 24.1 %copy-start = (bf16[64,24,128]{2,1,0:T(8,128)(2,1)S(1)}, bf16[64,24,128]{2,1,0:T(8,128)(2,1)}, u32[]{:S(2)}) copy-start(bf16[64,24,128]{2,1,0:T(8,128)(2,1)} %param.6) | copy-start | bytes 1179652
  25.7 20.5 %all-to-all-start.1 = ((bf16[128,24,128]{2,1,0:T(8,128)(2,1)}), bf16[128,24,128]{2,1,0:T(8,128)(2,1)S(1)}, u32[]{:S(2)}, u32[]{:S(2)}) async-start(bf16[128,24,128]{2,1,0:T(8,128)(2,1)} %gather_fusion), calls=%async_computation.1 | async-start | bytes 1572864 | tf_op jit(solution)/shard_map/all_to_all | solution.py:39
  72.4 6.4 %copy-start.2 = (s32[64,1]{0,1:T(1,128)S(1)}, s32[64,1]{0,1:T(1,128)}, u32[]{:S(2)}) copy-start(s32[64,1]{0,1:T(1,128)} %param.11) | copy-start | bytes 772
  74.0 26.2 %all-to-all-start.2 = ((f32[128,4,577]{2,1,0:T(4,128)}), f32[128,4,577]{2,1,0:T(4,128)S(1)}, u32[]{:S(2)}, u32[]{:S(2)}) async-start(f32[128,4,577]{2,1,0:T(4,128)} %copy.27), calls=%async_computation.2 | async-start | bytes 2621440 | tf_op jit(solution)/shard_map/all_to_all | solution.py:16
  213.5 2.2 %copy-start.1 = (bf16[64,24,128]{2,1,0:T(8,128)(2,1)S(1)}, bf16[64,24,128]{2,1,0:T(8,128)(2,1)}, u32[]{:S(2)}) copy-start(bf16[64,24,128]{2,1,0:T(8,128)(2,1)} %param.6) | copy-start | bytes 1179652
where the time goes:
time: 216 us
  blocking collectives  83.6 us (39%)
  matrix products  44 us (20%)
  local copies, waits for them, and re-layouts  39 us (18%)
  waiting for transfers between devices  35.5 us (16%)
  starting transfers between devices  9.28 us (4%)
  other arithmetic  4.17 us (2%)
    all_to_all x1, blocking collectives, per_device(): lax.all_to_all(outgoing, ('gx', 'gy'), split_axis=0, concat_axis=0, tiled...  62.7 us
    all_to_all x1, waiting for transfers between devices, side_by_side(): lax.all_to_all(both, axis, split_axis=split_dim, concat_axis=concat_dim,...  21.1 us
    all_to_all x1, blocking collectives, per_device(): lax.all_to_all(request, ('gx', 'gy'), split_axis=0, concat_axis=0, tiled=...  20.9 us
    dot_general x1, matrix products, placed(): jnp.einsum('tqce,tqn->tcne', partial_value, column_hot, precision=HIGH)  19 us
    transpose x1, local copies, waits for them, and re-layouts, placed(): jnp.einsum('tqce,tqn->tcne', partial_value, column_hot, precision=HIGH)  15.4 us
    all_to_all x1, waiting for transfers between devices, per_device(): lax.all_to_all(prolong[requested], ('gx', 'gy'), split_axis=0, concat_axi...  14.5 us
    dot_general x1, matrix products, per_device(): jnp.einsum('tqij,tqej->tqei', stiffness, col_rows, preferred_element_type...  12.8 us
    transpose x1, local copies, waits for them, and re-layouts, per_device(): jnp.einsum('tci,tqei->tqce', fetched.astype(jnp.float32), applied, precis...  5.46 us
  transfers between devices with their start and end apart: 2, of which 2 were waited for; matrix products, arithmetic and copies ran while one was open for 1% of the time, Pallas kernels for 0%

commit v1 on v0

v1 whole, which is shorter than its diff:
```python
import jax
import jax.numpy as jnp
from jax import lax
from jax.experimental import pallas as pl
from jax.experimental.pallas import tpu as pltpu
from jax.sharding import PartitionSpec as P

MAXNB = 16
AXES = ("gx", "gy")
F32 = jnp.float32
BF16 = jnp.bfloat16
I16 = jnp.int16
I32 = jnp.int32

TOP = 32766.0
TINY = 2.0**-120
LANES = 128
SUB = 32


def lane_ids(rows):
    return lax.broadcasted_iota(I32, (rows, LANES), 1)


def exponent(rows):
    top = jnp.maximum(jnp.max(jnp.abs(rows), axis=1, keepdims=True), TINY)
    return jnp.ceil(jnp.log2(top))


def gather_kernel(asked, prolong, out):
    def step(d, carry):
        out[d] = prolong[asked[d, 0, 0]]
        return carry

    lax.fori_loop(0, out.shape[0], step, 0, unroll=8)


def partial_kernel(slot, fetched, stiff, out, padded):
    block = stiff.shape[0]
    rows = fetched.shape[1]
    first = pl.program_id(0) * block
    per_row = stiff.shape[1]

    @pl.when(pl.program_id(0) == 0)
    def _():
        def fill(t, carry):
            padded[t, 0:rows, :] = fetched[t]
            padded[t, rows:SUB, :] = jnp.zeros((SUB - rows, LANES), BF16)
            return carry

        lax.fori_loop(0, fetched.shape[0], fill, 0, unroll=8)

    lanes = lane_ids(rows)
    for i in range(block):
        t = first + i
        mine = padded[t]
        stack = []
        for q in range(0, per_row, 2):
            pair = jnp.concatenate([stiff[i, q], stiff[i, q + 1]], axis=1)
            both = jnp.dot(mine, pair, preferred_element_type=F32)
            for h in range(2):
                w = both[0:rows, h * LANES : (h + 1) * LANES]
                high = w.astype(BF16).astype(F32)
                stack += [high, w - high]
        left = jnp.concatenate(stack, axis=0).astype(BF16)
        right = jnp.concatenate([padded[slot[q, t]] for q in range(per_row)], axis=0)
        prod = lax.dot_general(left, right, (((1,), (1,)), ((), ())), preferred_element_type=F32)
        value = jnp.zeros((rows, LANES), F32)
        for q in range(per_row):
            own = prod[2 * q * rows : (2 * q + 1) * rows] + prod[(2 * q + 1) * rows : (2 * q + 2) * rows]
            value = jnp.where(lanes // SUB == q, own, value)
        e = exponent(value)
        code = jnp.round(value * (jnp.exp2(-e) * TOP))
        code = jnp.where(lanes == rows, e, code)
        out[i] = code.astype(I16)


def place_kernel(asked, owner, blocks, out, acc):
    devices, rows, _ = blocks.shape
    aggs = acc.shape[0]
    tiles = acc.shape[2] // LANES
    lanes = lane_ids(rows)
    lane8 = lane_ids(8)

    def clear(a, carry):
        acc[a] = jnp.zeros(acc.shape[1:], F32)
        return carry

    lax.fori_loop(0, aggs, clear, 0, unroll=4)

    def clear_out(d, carry):
        out[d] = jnp.zeros(out.shape[1:], I16)
        return carry

    lax.fori_loop(0, devices, clear_out, 0, unroll=4)

    def add(d, carry):
        code = blocks[d].astype(F32)
        value = code * (jnp.exp2(code[:, rows : rows + 1]) * (1.0 / TOP))
        sums = [jnp.zeros((rows, LANES), F32) for _ in range(tiles)]
        for q in range(4):
            start = asked[d, 0, 1 + q] * rows
            turned = pltpu.roll(value, (start - q * SUB + LANES) % LANES, 1)
            for m in range(tiles):
                at = lanes + (m * LANES - start)
                sums[m] = jnp.where((at >= 0) & (at < rows), turned, sums[m])
        a = asked[d, 0, 0]
        for m in range(tiles):
            acc[a, :, m * LANES : (m + 1) * LANES] += sums[m]
        return carry

    lax.fori_loop(0, devices, add, 0, unroll=2)

    def send(a, carry):
        parts = []
        scales = jnp.zeros((8, LANES), F32)
        for m in range(tiles):
            value = acc[a, :, m * LANES : (m + 1) * LANES]
            e = exponent(value)
            parts.append(jnp.round(value * (jnp.exp2(-e) * TOP)))
            for r in range(rows // 8):
                scales = jnp.where(lane8 == m * (rows // 8) + r, e[8 * r : 8 * r + 8], scales)
        out[owner[0, a]] = jnp.concatenate(parts + [scales], axis=0).astype(I16)
        return carry

    lax.fori_loop(0, aggs, send, 0, unroll=2)


def decode_kernel(code, out):
    rows = out.shape[1]
    tiles = out.shape[2] // LANES
    bands = rows // 8
    for j in range(code.shape[0]):
        x = code[j].astype(F32)
        scales = jnp.exp2(x[rows * tiles : rows * tiles + 8]) * (1.0 / TOP)
        for m in range(tiles):
            for r in range(bands):
                i = m * bands + r
                out[j, 8 * r : 8 * r + 8, m * LANES : (m + 1) * LANES] = (
                    x[8 * i : 8 * i + 8] * scales[:, i : i + 1]
                )


def swap(x):
    return lax.all_to_all(x, AXES, split_axis=0, concat_axis=0, tiled=True)


def per_device(prolong, stiffness, request, col_slot, col_pos, coarse_owner):
    devices = lax.axis_size(AXES)
    aggs, rows, dof = prolong.shape
    per_row = stiffness.shape[1]
    width = MAXNB * rows
    smem = pl.BlockSpec(memory_space=pltpu.SMEM)

    asking = jnp.concatenate([request[:, None], col_pos], axis=1)[:, None, :]
    asked = swap(asking)

    picked = pl.pallas_call(
        gather_kernel,
        out_shape=jax.ShapeDtypeStruct((devices, rows, dof), BF16),
        in_specs=[smem, pl.BlockSpec(memory_space=pltpu.VMEM)],
        out_specs=pl.BlockSpec(memory_space=pltpu.VMEM),
        name="pick",
    )(asked, prolong)
    fetched = swap(picked)

    block = 8
    sent = pl.pallas_call(
        partial_kernel,
        grid=(devices // block,),
        out_shape=jax.ShapeDtypeStruct((devices, rows, LANES), I16),
        in_specs=[
            smem,
            pl.BlockSpec((devices, rows, dof), lambda g: (0, 0, 0)),
            pl.BlockSpec((block, per_row, dof, dof), lambda g: (g, 0, 0, 0)),
        ],
        out_specs=pl.BlockSpec((block, rows, LANES), lambda g: (g, 0, 0)),
        scratch_shapes=[pltpu.VMEM((devices, SUB, dof), BF16)],
        name="partial",
    )(col_slot.T, fetched, stiffness)
    blocks = swap(sent)

    depth = rows * (width // LANES) + 8
    rows_out = pl.pallas_call(
        place_kernel,
        out_shape=jax.ShapeDtypeStruct((devices, depth, LANES), I16),
        in_specs=[smem, smem, pl.BlockSpec(memory_space=pltpu.VMEM)],
        out_specs=pl.BlockSpec(memory_space=pltpu.VMEM),
        scratch_shapes=[pltpu.VMEM((aggs, rows, width), F32)],
        name="place",
    )(asked, coarse_owner.T, blocks)
    arrived = swap(rows_out)

    step = 16
    return pl.pallas_call(
        decode_kernel,
        grid=(devices // step,),
        out_shape=jax.ShapeDtypeStruct((devices, rows, width), F32),
        in_specs=[pl.BlockSpec((step, depth, LANES), lambda g: (g, 0, 0))],
        out_specs=pl.BlockSpec((step, rows, width), lambda g: (g, 0, 0)),
        name="decode",
    )(arrived)


def solution(mesh):
    placed = (
        P(AXES, None, None),
        P(AXES, None, None, None),
        P(AXES),
        P(AXES, None),
        P(AXES, None),
        P(AXES, None),
    )
    return jax.shard_map(
        per_device, mesh=mesh, in_specs=placed, out_specs=P(AXES, None, None), check_vma=False
    )
```

time: 216 us -> 154 us (0.71)
  Pallas kernels: 0 us -> 46.6 us
  matrix products: 44 us -> 0 us
  local copies, waits for them, and re-layouts: 39 us -> 0.11 us
  waiting for transfers between devices: 35.5 us -> 0 us
  blocking collectives: 83.6 us -> 106 us
  starting transfers between devices: 9.28 us -> 0 us
  other arithmetic: 4.17 us -> 0.69 us
    pallas_call x0 -> x4, Pallas kernels: none -> 46.6 us  [the longest x1 19.1 us: per_device(): pl.pallas_call(place_kernel, out_shape=jax.ShapeDtypeStruct((devices, dep...]
    dot_general x5 -> x0, matrix products: 44 us -> none  [the longest x1 19 us: placed(): jnp.einsum('tqce,tqn->tcne', partial_value, column_hot, precision=HIGH)]
    all_to_all x2 -> x0, waiting for transfers between devices: 35.5 us -> none  [the longest x1 21.1 us: side_by_side(): lax.all_to_all(both, axis, split_axis=split_dim, concat_axis=concat_dim,...]
    all_to_all x2 -> x4, blocking collectives: 83.6 us -> 106 us  [swap(): return lax.all_to_all(x, AXES, split_axis=0, concat_axis=0, tiled=True)]
    transpose x2 -> x0, local copies, waits for them, and re-layouts: 20.9 us -> none  [the longest x1 15.4 us: placed(): jnp.einsum('tqce,tqn->tcne', partial_value, column_hot, precision=HIGH)]
    all_to_all x2 -> x0, starting transfers between devices: 9.28 us -> none  [the longest x1 4.8 us: side_by_side(): lax.all_to_all(both, axis, split_axis=split_dim, concat_axis=concat_dim,...]
    gather x2 -> x0, local copies, waits for them, and re-layouts: 4.73 us -> none  [the longest x1 3.15 us: per_device(): col_rows = fetched[col_slot]]
    reshape x1 -> x0, local copies, waits for them, and re-layouts: 4.64 us -> none  [side_by_side(): done.append(slab.reshape(*slab.shape[:along], *a.shape[along:]))]
  transfers between devices with their start and end apart: 2 -> 0, of which waited for: 2 -> 0; matrix products, arithmetic and copies ran while one was open for 1% -> 0% of each run, Pallas kernels for 0% -> 0%
where the time goes in v1:
time: 154 us; the launch traced here: 153 us
  blocking collectives  106 us (69%)
  Pallas kernels  46.6 us (30%)
    all_to_all x4, blocking collectives, swap(): return lax.all_to_all(x, AXES, split_axis=0, concat_axis=0, tiled=True)  106 us
    pallas_call x1, Pallas kernels, per_device(): pl.pallas_call(place_kernel, out_shape=jax.ShapeDtypeStruct((devices, dep...  19.1 us
    pallas_call x1, Pallas kernels, per_device(): pl.pallas_call(partial_kernel, grid=(devices // block,), out_shape=jax.Sh...  17.3 us
    pallas_call x1, Pallas kernels, per_device(): pl.pallas_call(decode_kernel, grid=(devices // step,), out_shape=jax.Shap...  7.33 us

profile of v1, /device:TPU:1, one launch (start us, length us, event | category | flops | bytes accessed | tf_op | source)
XLA Modules:
  0.0 153.3 jit_solution(3176575492581837593)
XLA Ops:
  0.0 0.7 pad_add_fusion
  0.7 0.1 copy.9
  0.8 21.3 %all_to_all.20.asked = s32[128,1,5]{2,1,0:T(1,128)} all-to-all(s32[128,1,5]{2,1,0:T(1,128)S(1)} %bitcast.4), channel_id=1, replica_groups=mesh['gx'=8,'gy'=16] {'gx','gy'}, dimensions={0} | all-to-all | bytes 5120 | tf_op jit(solution)/shard_map/all_to_all | solution.py:145
  22.1 2.9 %pick.1 = bf16[128,24,128]{2,1,0:T(8,128)(2,1)} custom-call(s32[128,1,5]{2,1,0:T(1,128)} %all_to_all.20.asked, bf16[64,24,128]{2,1,0:T(8,128)(2,1)} %prolong.1), custom_call_target="tpu_custom_call" | custom-call | tf_op jit(solution)/shard_map/pick/pallas_call | solution.py:158
  25.0 21.5 %all_to_all.21.fetched = bf16[128,24,128]{2,1,0:T(8,128)(2,1)} all-to-all(bf16[128,24,128]{2,1,0:T(8,128)(2,1)} %pick.1), channel_id=1, replica_groups=mesh['gx'=8,'gy'=16] {'gx','gy'}, dimensions={0} | all-to-all | bytes 1572864 | tf_op jit(solution)/shard_map/all_to_all | solution.py:145
  46.5 17.3 %partial.1 = s16[128,24,128]{2,1,0:T(8,128)(2,1)} custom-call(s32[4,128]{1,0:T(4,128)} %bitcast.5, bf16[128,24,128]{2,1,0:T(8,128)(2,1)} %all_to_all.21.fetched, bf16[128,4,128,128]{3,2,1,0:T(8,128)(2,1)} %stiff.1), custom_call_target="tpu_custom_call" | custom-call | tf_op jit(solution)/shard_map/partial/pallas_call | solution.py:168
  63.8 21.9 %all_to_all.22.blocks = s16[128,24,128]{2,1,0:T(8,128)(2,1)} all-to-all(s16[128,24,128]{2,1,0:T(8,128)(2,1)} %partial.1), channel_id=1, replica_groups=mesh['gx'=8,'gy'=16] {'gx','gy'}, dimensions={0} | all-to-all | bytes 1572864 | tf_op jit(solution)/shard_map/all_to_all | solution.py:145
  85.7 19.1 %place.1 = s16[128,80,128]{2,1,0:T(8,128)(2,1)} custom-call(s32[128,1,5]{2,1,0:T(1,128)} %all_to_all.20.asked, s32[1,64]{1,0:T(1,128)} %bitcast.6, s16[128,24,128]{2,1,0:T(8,128)(2,1)} %all_to_all.22.blocks), custom_call_target="tpu_custom_call" | custom-call | tf_op jit(solution)/shard_map/place/pallas_call | solution.py:184
  104.8 41.2 %all_to_all.23.code = s16[128,80,128]{2,1,0:T(8,128)(2,1)} all-to-all(s16[128,80,128]{2,1,0:T(8,128)(2,1)} %place.1), channel_id=1, replica_groups=mesh['gx'=8,'gy'=16] {'gx','gy'}, dimensions={0} | all-to-all | bytes 5242880 | tf_op jit(solution)/shard_map/all_to_all | solution.py:145
  146.0 7.3 %decode.1 = f32[128,24,384]{2,1,0:T(8,128)} custom-call(s16[128,80,128]{2,1,0:T(8,128)(2,1)} %all_to_all.23.code), custom_call_target="tpu_custom_call" | custom-call | tf_op jit(solution)/shard_map/decode/pallas_call | solution.py:195

commit v2 on v1

v2 whole, which is shorter than its diff:
```python
import jax
import jax.numpy as jnp
from jax import lax
from jax.experimental import pallas as pl
from jax.experimental.pallas import tpu as pltpu
from jax.sharding import PartitionSpec as P

MAXNB = 16
AXES = ("gx", "gy")
F32 = jnp.float32
BF16 = jnp.bfloat16
I16 = jnp.int16
I32 = jnp.int32

TOP = 32766.0
TINY = 2.0**-120
LANES = 128
SUB = 32


def lane_ids(rows):
    return lax.broadcasted_iota(I32, (rows, LANES), 1)


def level(top):
    return jnp.ceil(8.0 * jnp.log2(jnp.maximum(top, TINY)))


def gather_kernel(asked, prolong, out):
    def step(d, carry):
        out[d] = prolong[asked[d, 0, 0]]
        return carry

    lax.fori_loop(0, out.shape[0], step, 0, unroll=16)


def partial_kernel(slot, fetched, stiff, out, padded):
    block = stiff.shape[0]
    rows = fetched.shape[1]
    first = pl.program_id(0) * block
    per_row = stiff.shape[1]

    @pl.when(pl.program_id(0) == 0)
    def _():
        def fill(t, carry):
            padded[t, 0:rows, :] = fetched[t]
            padded[t, rows:SUB, :] = jnp.zeros((SUB - rows, LANES), BF16)
            return carry

        lax.fori_loop(0, fetched.shape[0], fill, 0, unroll=8)

    lanes = lane_ids(rows)
    for i in range(block):
        t = first + i
        mine = padded[t]
        highs = []
        lows = []
        for q in range(0, per_row, 2):
            pair = jnp.concatenate([stiff[i, q], stiff[i, q + 1]], axis=1)
            both = jnp.dot(mine, pair, preferred_element_type=F32)
            for h in range(2):
                w = both[0:rows, h * LANES : (h + 1) * LANES]
                high = w.astype(BF16).astype(F32)
                highs.append(high)
                lows.append(w - high)
        left = jnp.concatenate(
            [jnp.concatenate(highs, axis=0).astype(BF16), jnp.concatenate(lows, axis=0).astype(BF16)], axis=1
        )
        right = jnp.concatenate([padded[slot[q, t]] for q in range(per_row)], axis=0)
        right = jnp.concatenate([right, right], axis=1)
        prod = lax.dot_general(left, right, (((1,), (1,)), ((), ())), preferred_element_type=F32)
        value = prod[0:rows]
        for q in range(1, per_row):
            value = jnp.where(lanes < q * SUB, value, prod[q * rows : (q + 1) * rows])
        e = level(jnp.max(jnp.abs(value), axis=1, keepdims=True))
        code = jnp.round(value * (jnp.exp2(e * -0.125) * TOP))
        code = jnp.where(lanes == rows, e, code)
        out[i] = code.astype(I16)


def place_kernel(asked, owner, blocks, out, acc):
    devices, rows, _ = blocks.shape
    aggs = acc.shape[0]
    tiles = acc.shape[2] // LANES
    lanes = lane_ids(8)
    bands = rows // 8
    sub8 = lax.broadcasted_iota(I32, (8, LANES), 0)

    def clear(a, carry):
        acc[a] = jnp.zeros(acc.shape[1:], F32)
        return carry

    lax.fori_loop(0, aggs, clear, 0, unroll=8)

    def clear_out(d, carry):
        out[d] = jnp.zeros(out.shape[1:], I16)
        return carry

    lax.fori_loop(0, devices, clear_out, 0, unroll=8)

    def add(d, carry):
        code = blocks[d].astype(F32)
        scale = jnp.exp2(code[:, rows : rows + 1] * 0.125) * (1.0 / TOP)
        sums = [jnp.zeros((rows, LANES), F32) for _ in range(tiles)]
        for q in range(4):
            start = asked[d, 0, 1 + q]
            turned = pltpu.roll(code, (start - q * SUB + LANES) & (LANES - 1), 1)
            for m in range(tiles):
                at = (lanes + m * LANES) - start
                inside = at.astype(jnp.uint32) < rows
                inside = jnp.concatenate([inside] * bands, axis=0)
                sums[m] = jnp.where(inside, turned, sums[m])
        a = asked[d, 0, 0]
        for m in range(tiles):
            acc[a, :, m * LANES : (m + 1) * LANES] += sums[m] * scale
        return carry

    lax.fori_loop(0, devices, add, 0, unroll=8)

    def send(a, carry):
        parts = []
        scales = jnp.zeros((8, LANES), F32)
        for m in range(tiles):
            value = acc[a, :, m * LANES : (m + 1) * LANES]
            e = level(jnp.max(jnp.abs(value), axis=0, keepdims=True))
            parts.append(jnp.round(value * (jnp.exp2(e * -0.125) * TOP)))
            scales = jnp.where(sub8 == m, e, scales)
        out[owner[0, a]] = jnp.concatenate(parts + [scales], axis=0).astype(I16)
        return carry

    lax.fori_loop(0, aggs, send, 0, unroll=8)


def decode_kernel(code, out):
    rows = out.shape[1]
    tiles = out.shape[2] // LANES
    for j in range(code.shape[0]):
        x = code[j].astype(F32)
        scales = jnp.exp2(x[rows * tiles : rows * tiles + 8] * 0.125) * (1.0 / TOP)
        for m in range(tiles):
            out[j, :, m * LANES : (m + 1) * LANES] = x[rows * m : rows * (m + 1)] * scales[m : m + 1]


def swap(x):
    return lax.all_to_all(x, AXES, split_axis=0, concat_axis=0, tiled=True)


def per_device(prolong, stiffness, request, col_slot, col_pos, coarse_owner):
    devices = lax.axis_size(AXES)
    aggs, rows, dof = prolong.shape
    per_row = stiffness.shape[1]
    width = MAXNB * rows
    smem = pl.BlockSpec(memory_space=pltpu.SMEM)

    asking = jnp.concatenate([request[:, None], col_pos * rows], axis=1)[:, None, :]
    asked = swap(asking)

    picked = pl.pallas_call(
        gather_kernel,
        out_shape=jax.ShapeDtypeStruct((devices, rows, dof), BF16),
        in_specs=[smem, pl.BlockSpec(memory_space=pltpu.VMEM)],
        out_specs=pl.BlockSpec(memory_space=pltpu.VMEM),
        name="pick",
        compiler_params=pltpu.CompilerParams(vmem_limit_bytes=4 << 20),
    )(asked, prolong)
    fetched = swap(picked)

    block = 32
    sent = pl.pallas_call(
        partial_kernel,
        grid=(devices // block,),
        out_shape=jax.ShapeDtypeStruct((devices, rows, LANES), I16),
        in_specs=[
            smem,
            pl.BlockSpec((devices, rows, dof), lambda g: (0, 0, 0)),
            pl.BlockSpec((block, per_row, dof, dof), lambda g: (g, 0, 0, 0)),
        ],
        out_specs=pl.BlockSpec((block, rows, LANES), lambda g: (g, 0, 0)),
        scratch_shapes=[pltpu.VMEM((devices, SUB, dof), BF16)],
        name="partial",
        compiler_params=pltpu.CompilerParams(vmem_limit_bytes=48 << 20),
    )(col_slot.T, fetched, stiffness)
    blocks = swap(sent)

    depth = rows * (width // LANES) + 8
    rows_out = pl.pallas_call(
        place_kernel,
        out_shape=jax.ShapeDtypeStruct((devices, depth, LANES), I16),
        in_specs=[smem, smem, pl.BlockSpec(memory_space=pltpu.VMEM)],
        out_specs=pl.BlockSpec(memory_space=pltpu.VMEM),
        scratch_shapes=[pltpu.VMEM((aggs, rows, width), F32)],
        name="place",
        compiler_params=pltpu.CompilerParams(vmem_limit_bytes=16 << 20),
    )(asked, coarse_owner.T, blocks)
    arrived = swap(rows_out)

    step = 16
    return pl.pallas_call(
        decode_kernel,
        grid=(devices // step,),
        out_shape=jax.ShapeDtypeStruct((devices, rows, width), F32),
        in_specs=[pl.BlockSpec((step, depth, LANES), lambda g: (g, 0, 0))],
        out_specs=pl.BlockSpec((step, rows, width), lambda g: (g, 0, 0)),
        name="decode",
        compiler_params=pltpu.CompilerParams(vmem_limit_bytes=16 << 20),
    )(arrived)


def solution(mesh):
    placed = (
        P(AXES, None, None),
        P(AXES, None, None, None),
        P(AXES),
        P(AXES, None),
        P(AXES, None),
        P(AXES, None),
    )
    return jax.shard_map(
        per_device, mesh=mesh, in_specs=placed, out_specs=P(AXES, None, None), check_vma=False
    )
```

time: 154 us -> 126 us (0.82)
  Pallas kernels: 46.6 us -> 21 us
  blocking collectives: 106 us -> 101 us
  local copies, waits for them, and re-layouts: 0.11 us -> 1.8 us
    pallas_call x1, Pallas kernels: 19.1 us -> 6.33 us  [per_device(): pl.pallas_call(place_kernel, out_shape=jax.ShapeDtypeStruct((devices, dep...]
    pallas_call x1, Pallas kernels: 17.3 us -> 9.13 us  [per_device(): pl.pallas_call(partial_kernel, grid=(devices // block,), out_shape=jax.Sh...]
    all_to_all x4, blocking collectives: 106 us -> 101 us  [swap(): return lax.all_to_all(x, AXES, split_axis=0, concat_axis=0, tiled=True)]
    pallas_call x1, Pallas kernels: 7.33 us -> 3.77 us  [per_device(): pl.pallas_call(decode_kernel, grid=(devices // step,), out_shape=jax.Shap...]
    unnamed x0 -> x6, local copies, waits for them, and re-layouts: none -> 1.68 us
where the time goes in v2:
time: 126 us; the launch traced here: 125 us
  blocking collectives  101 us (80%)
  Pallas kernels  21 us (17%)
  local copies, waits for them, and re-layouts  1.8 us (1%)
  other arithmetic  1.35 us (1%)
    all_to_all x4, blocking collectives, swap(): return lax.all_to_all(x, AXES, split_axis=0, concat_axis=0, tiled=True)  101 us
    pallas_call x1, Pallas kernels, per_device(): pl.pallas_call(partial_kernel, grid=(devices // block,), out_shape=jax.Sh...  9.13 us
    pallas_call x1, Pallas kernels, per_device(): pl.pallas_call(place_kernel, out_shape=jax.ShapeDtypeStruct((devices, dep...  6.33 us
    pallas_call x1, Pallas kernels, per_device(): pl.pallas_call(decode_kernel, grid=(devices // step,), out_shape=jax.Shap...  3.77 us

profile of v2, /device:TPU:1, one launch (start us, length us, event | category | flops | bytes accessed | tf_op | source)
XLA Modules:
  0.0 125.5 jit_solution(1526450363284289928)
XLA Ops:
  0.0 0.7 broadcast_multiply_fusion
  0.7 0.7 pad_add_fusion
  1.3 0.1 copy.10
  1.5 20.9 %all_to_all.20.asked = s32[128,1,5]{2,1,0:T(1,128)S(1)} all-to-all(s32[128,1,5]{2,1,0:T(1,128)S(1)} %bitcast.6), channel_id=1, replica_groups=mesh['gx'=8,'gy'=16] {'gx','gy'}, dimensions={0} | all-to-all | bytes 5120 | tf_op jit(solution)/shard_map/all_to_all | solution.py:145
  22.4 0.0 copy-start
  22.4 1.0 copy-done
  23.4 1.8 %pick.1 = bf16[128,24,128]{2,1,0:T(8,128)(2,1)S(1)} custom-call(s32[128,1,5]{2,1,0:T(1,128)S(1)} %all_to_all.20.asked, bf16[64,24,128]{2,1,0:T(8,128)(2,1)S(1)} %copy-done), custom_call_target="tpu_custom_call" | custom-call | tf_op jit(solution)/shard_map/pick/pallas_call | solution.py:158
  25.2 20.3 %all_to_all.21.fetched = bf16[128,24,128]{2,1,0:T(8,128)(2,1)S(1)} all-to-all(bf16[128,24,128]{2,1,0:T(8,128)(2,1)S(1)} %pick.1), channel_id=1, replica_groups=mesh['gx'=8,'gy'=16] {'gx','gy'}, dimensions={0} | all-to-all | bytes 1572864 | tf_op jit(solution)/shard_map/all_to_all | solution.py:145
  45.5 0.0 copy-start.1
  45.5 0.7 copy-done.1
  46.2 0.0 copy-start.2
  46.2 9.1 %partial.1 = s16[128,24,128]{2,1,0:T(8,128)(2,1)S(1)} custom-call(s32[4,128]{1,0:T(4,128)S(1)} %bitcast.4, bf16[128,24,128]{2,1,0:T(8,128)(2,1)S(1)} %all_to_all.21.fetched, bf16[128,4,128,128]{3,2,1,0:T(8,128)(2,1)} %stiff.1), custom_call_target="tpu_custom_call" | custom-call | tf_op jit(solution)/shard_map/partial/pallas_call | solution.py:169
  55.3 20.4 %all_to_all.22.blocks = s16[128,24,128]{2,1,0:T(8,128)(2,1)S(1)} all-to-all(s16[128,24,128]{2,1,0:T(8,128)(2,1)S(1)} %partial.1), channel_id=1, replica_groups=mesh['gx'=8,'gy'=16] {'gx','gy'}, dimensions={0} | all-to-all | bytes 1572864 | tf_op jit(solution)/shard_map/all_to_all | solution.py:145
  75.6 0.0 copy-done.2
  75.7 6.3 %place.1 = s16[128,80,128]{2,1,0:T(8,128)(2,1)S(1)} custom-call(s32[128,1,5]{2,1,0:T(1,128)S(1)} %all_to_all.20.asked, s32[1,64]{1,0:T(1,128)S(1)} %bitcast.5, s16[128,24,128]{2,1,0:T(8,128)(2,1)S(1)} %all_to_all.22.blocks), custom_call_target="tpu_custom_call" | custom-call | tf_op jit(solution)/shard_map/place/pallas_call | solution.py:186
  82.0 39.7 %all_to_all.23.code = s16[128,80,128]{2,1,0:T(8,128)(2,1)S(1)} all-to-all(s16[128,80,128]{2,1,0:T(8,128)(2,1)S(1)} %place.1), channel_id=1, replica_groups=mesh['gx'=8,'gy'=16] {'gx','gy'}, dimensions={0} | all-to-all | bytes 5242880 | tf_op jit(solution)/shard_map/all_to_all | solution.py:145
  121.7 3.8 %decode.1 = f32[128,24,384]{2,1,0:T(8,128)} custom-call(s16[128,80,128]{2,1,0:T(8,128)(2,1)S(1)} %all_to_all.23.code), custom_call_target="tpu_custom_call" | custom-call | tf_op jit(solution)/shard_map/decode/pallas_call | solution.py:198
Async XLA Ops:
  22.4 1.0 copy-start
  45.5 0.7 copy-start.1
  46.2 29.5 %copy-start.2 = (s32[64,1]{0,1:T(1,128)S(1)}, s32[64,1]{0,1:T(1,128)}, u32[]{:S(2)}) copy-start(s32[64,1]{0,1:T(1,128)} %param.11) | copy-start | bytes 772

commit v3 on v2

--- a/solution.py
+++ b/solution.py
@@ -26,6 +26,14 @@
     return jnp.ceil(8.0 * jnp.log2(jnp.maximum(top, TINY)))
 
 
+def prep_kernel(request, col_pos, prolong, asking, held, sem):
+    copy = pltpu.make_async_copy(prolong, held, sem)
+    copy.start()
+    heads = jnp.concatenate([request[...], col_pos[...], jnp.zeros((3, LANES), I32)], axis=0)
+    asking[...] = heads.T
+    copy.wait()
+
+
 def gather_kernel(asked, prolong, out):
     def step(d, carry):
         out[d] = prolong[asked[d, 0, 0]]
@@ -34,25 +42,16 @@
     lax.fori_loop(0, out.shape[0], step, 0, unroll=16)
 
 
-def partial_kernel(slot, fetched, stiff, out, padded):
+def partial_kernel(slot, fetched, stiff, out, padded, terms):
     block = stiff.shape[0]
     rows = fetched.shape[1]
-    first = pl.program_id(0) * block
+    g = pl.program_id(0)
+    last = pl.num_programs(0) - 1
     per_row = stiff.shape[1]
-
-    @pl.when(pl.program_id(0) == 0)
-    def _():
-        def fill(t, carry):
-            padded[t, 0:rows, :] = fetched[t]
-            padded[t, rows:SUB, :] = jnp.zeros((SUB - rows, LANES), BF16)
-            return carry
-
-        lax.fori_loop(0, fetched.shape[0], fill, 0, unroll=8)
-
     lanes = lane_ids(rows)
-    for i in range(block):
-        t = first + i
-        mine = padded[t]
+
+    def left_product(i):
+        mine = padded[g * block + i]
         highs = []
         lows = []
         for q in range(0, per_row, 2):
@@ -63,12 +62,14 @@
                 high = w.astype(BF16).astype(F32)
                 highs.append(high)
                 lows.append(w - high)
-        left = jnp.concatenate(
-            [jnp.concatenate(highs, axis=0).astype(BF16), jnp.concatenate(lows, axis=0).astype(BF16)], axis=1
-        )
+        terms[i, :, 0:LANES] = jnp.concatenate(highs, axis=0).astype(BF16)
+        terms[i, :, LANES : 2 * LANES] = jnp.concatenate(lows, axis=0).astype(BF16)
+
+    def right_product(i):
+        t = (g - 1) * block + i
         right = jnp.concatenate([padded[slot[q, t]] for q in range(per_row)], axis=0)
         right = jnp.concatenate([right, right], axis=1)
-        prod = lax.dot_general(left, right, (((1,), (1,)), ((), ())), preferred_element_type=F32)
+        prod = lax.dot_general(terms[i], right, (((1,), (1,)), ((), ())), preferred_element_type=F32)
         value = prod[0:rows]
         for q in range(1, per_row):
             value = jnp.where(lanes < q * SUB, value, prod[q * rows : (q + 1) * rows])
@@ -77,6 +78,28 @@
         code = jnp.where(lanes == rows, e, code)
         out[i] = code.astype(I16)
 
+    @pl.when(g == 0)
+    def _():
+        def fill(t, carry):
+            padded[t, 0:rows, :] = fetched[t]
+            padded[t, rows:SUB, :] = jnp.zeros((SUB - rows, LANES), BF16)
+            return carry
+
+        lax.fori_loop(0, fetched.shape[0], fill, 0, unroll=8)
+        for i in range(block):
+            left_product(i)
+
+    @pl.when((g > 0) & (g < last))
+    def _():
+        for i in range(block):
+            right_product(i)
+            left_product(i)
+
+    @pl.when(g == last)
+    def _():
+        for i in range(block):
+            right_product(i)
+
 
 def place_kernel(asked, owner, blocks, out, acc):
     devices, rows, _ = blocks.shape
@@ -103,7 +126,7 @@
         scale = jnp.exp2(code[:, rows : rows + 1] * 0.125) * (1.0 / TOP)
         sums = [jnp.zeros((rows, LANES), F32) for _ in range(tiles)]
         for q in range(4):
-            start = asked[d, 0, 1 + q]
+            start = asked[d, 0, 1 + q] * rows
             turned = pltpu.roll(code, (start - q * SUB + LANES) & (LANES - 1), 1)
             for m in range(tiles):
                 at = (lanes + m * LANES) - start
@@ -145,6 +168,10 @@
     return lax.all_to_all(x, AXES, split_axis=0, concat_axis=0, tiled=True)
 
 
+def in_hbm(x):
+    return pltpu.with_memory_space_constraint(x, pltpu.HBM)
+
+
 def per_device(prolong, stiffness, request, col_slot, col_pos, coarse_owner):
     devices = lax.axis_size(AXES)
     aggs, rows, dof = prolong.shape
@@ -152,8 +179,20 @@
     width = MAXNB * rows
     smem = pl.BlockSpec(memory_space=pltpu.SMEM)
 
-    asking = jnp.concatenate([request[:, None], col_pos * rows], axis=1)[:, None, :]
-    asked = swap(asking)
+    vmem = pl.BlockSpec(memory_space=pltpu.VMEM)
+    asking, held = pl.pallas_call(
+        prep_kernel,
+        out_shape=(
+            jax.ShapeDtypeStruct((devices, 8), I32),
+            jax.ShapeDtypeStruct((aggs, rows, dof), BF16),
+        ),
+        in_specs=[vmem, vmem, pl.BlockSpec(memory_space=pltpu.HBM)],
+        out_specs=(vmem, vmem),
+        scratch_shapes=[pltpu.SemaphoreType.DMA],
+        compiler_params=pltpu.CompilerParams(vmem_limit_bytes=4 << 20),
+        name="prep",
+    )(in_hbm(request[None, :]), in_hbm(col_pos.T), in_hbm(prolong))
+    asked = swap(asking[:, None, :])
 
     picked = pl.pallas_call(
         gather_kernel,
@@ -162,24 +201,28 @@
         out_specs=pl.BlockSpec(memory_space=pltpu.VMEM),
         name="pick",
         compiler_params=pltpu.CompilerParams(vmem_limit_bytes=4 << 20),
-    )(asked, prolong)
+    )(asked, held)
     fetched = swap(picked)
 
-    block = 32
+    block = 16
+    steps = devices // block
     sent = pl.pallas_call(
         partial_kernel,
-        grid=(devices // block,),
+        grid=(steps + 1,),
         out_shape=jax.ShapeDtypeStruct((devices, rows, LANES), I16),
         in_specs=[
             smem,
             pl.BlockSpec((devices, rows, dof), lambda g: (0, 0, 0)),
-            pl.BlockSpec((block, per_row, dof, dof), lambda g: (g, 0, 0, 0)),
+            pl.BlockSpec((block, per_row, dof, dof), lambda g: (jnp.minimum(g, steps - 1), 0, 0, 0)),
         ],
-        out_specs=pl.BlockSpec((block, rows, LANES), lambda g: (g, 0, 0)),
-        scratch_shapes=[pltpu.VMEM((devices, SUB, dof), BF16)],
+        out_specs=pl.BlockSpec((block, rows, LANES), lambda g: (jnp.maximum(g - 1, 0), 0, 0)),
+        scratch_shapes=[
+            pltpu.VMEM((devices, SUB, dof), BF16),
+            pltpu.VMEM((block, rows * per_row, 2 * dof), BF16),
+        ],
         name="partial",
         compiler_params=pltpu.CompilerParams(vmem_limit_bytes=48 << 20),
-    )(col_slot.T, fetched, stiffness)
+    )(in_hbm(col_slot.T), fetched, stiffness)
     blocks = swap(sent)
 
     depth = rows * (width // LANES) + 8
@@ -191,10 +234,10 @@
         scratch_shapes=[pltpu.VMEM((aggs, rows, width), F32)],
         name="place",
         compiler_params=pltpu.CompilerParams(vmem_limit_bytes=16 << 20),
-    )(asked, coarse_owner.T, blocks)
+    )(asked, in_hbm(coarse_owner.T), blocks)
     arrived = swap(rows_out)
 
-    step = 16
+    step = 32
     return pl.pallas_call(
         decode_kernel,
         grid=(devices // step,),

time: 126 us -> 126 us (level)
  Pallas kernels: 21 us -> 24.1 us
  local copies, waits for them, and re-layouts: 1.8 us -> 0 us
  other arithmetic: 1.35 us -> 0 us
    pallas_call x1 -> x2, Pallas kernels: 9.13 us -> 13.1 us  [the longest x1 11.4 us: per_device(): pl.pallas_call(partial_kernel, grid=(steps + 1,), out_shape=jax.ShapeDtyp...]
    unnamed x6 -> x0, local copies, waits for them, and re-layouts: 1.68 us -> none
where the time goes in v3:
time: 126 us; the launch traced here: 125 us
  blocking collectives  101 us (80%)
  Pallas kernels  24.1 us (19%)
    all_to_all x4, blocking collectives, swap(): return lax.all_to_all(x, AXES, split_axis=0, concat_axis=0, tiled=True)  101 us
    pallas_call x1, Pallas kernels, per_device(): pl.pallas_call(partial_kernel, grid=(steps + 1,), out_shape=jax.ShapeDtyp...  11.4 us
    pallas_call x1, Pallas kernels, per_device(): pl.pallas_call(place_kernel, out_shape=jax.ShapeDtypeStruct((devices, dep...  6.46 us
    pallas_call x1, Pallas kernels, per_device(): pl.pallas_call(decode_kernel, grid=(devices // step,), out_shape=jax.Shap...  2.72 us

profile of v3, /device:TPU:1, one launch (start us, length us, event | category | flops | bytes accessed | tf_op | source)
XLA Modules:
  0.0 125.3 jit_solution(1478237946644452326)
XLA Ops:
  0.0 1.7 %prep.1 = (s32[128,8]{1,0:T(8,128)S(1)}, bf16[64,24,128]{2,1,0:T(8,128)(2,1)S(1)}) custom-call(s32[1,128]{1,0:T(1,128)} %bitcast.8, s32[4,128]{1,0:T(4,128)} %bitcast.6, bf16[64,24,128]{2,1,0:T(8,128)(2,1)} %prolong.1), custom_call_target="tpu_custom_call" | custom-call | tf_op jit(solution)/shard_map/prep/pallas_call | solution.py:183
  1.7 20.9 %all_to_all.20.asked = s32[128,1,8]{2,1,0:T(1,128)S(1)} all-to-all(s32[128,1,8]{2,1,0:T(1,128)S(1)} %bitcast.5), channel_id=1, replica_groups=mesh['gx'=8,'gy'=16] {'gx','gy'}, dimensions={0} | all-to-all | bytes 8192 | tf_op jit(solution)/shard_map/all_to_all | solution.py:168
  22.6 1.8 %pick.1 = bf16[128,24,128]{2,1,0:T(8,128)(2,1)S(1)} custom-call(s32[128,1,8]{2,1,0:T(1,128)S(1)} %all_to_all.20.asked, bf16[64,24,128]{2,1,0:T(8,128)(2,1)S(1)} %get-tuple-element.8.prolong), custom_call_target="tpu_custom_call" | custom-call | tf_op jit(solution)/shard_map/pick/pallas_call | solution.py:197
  24.4 20.3 %all_to_all.21.fetched = bf16[128,24,128]{2,1,0:T(8,128)(2,1)S(1)} all-to-all(bf16[128,24,128]{2,1,0:T(8,128)(2,1)S(1)} %pick.1), channel_id=1, replica_groups=mesh['gx'=8,'gy'=16] {'gx','gy'}, dimensions={0} | all-to-all | bytes 1572864 | tf_op jit(solution)/shard_map/all_to_all | solution.py:168
  44.7 11.4 %partial.1 = s16[128,24,128]{2,1,0:T(8,128)(2,1)S(1)} custom-call(s32[4,128]{1,0:T(4,128)} %bitcast.7, bf16[128,24,128]{2,1,0:T(8,128)(2,1)S(1)} %all_to_all.21.fetched, bf16[128,4,128,128]{3,2,1,0:T(8,128)(2,1)} %stiff.1), custom_call_target="tpu_custom_call" | custom-call | tf_op jit(solution)/shard_map/partial/pallas_call | solution.py:209
  56.1 20.3 %all_to_all.22.blocks = s16[128,24,128]{2,1,0:T(8,128)(2,1)S(1)} all-to-all(s16[128,24,128]{2,1,0:T(8,128)(2,1)S(1)} %partial.1), channel_id=1, replica_groups=mesh['gx'=8,'gy'=16] {'gx','gy'}, dimensions={0} | all-to-all | bytes 1572864 | tf_op jit(solution)/shard_map/all_to_all | solution.py:168
  76.5 6.5 %place.1 = s16[128,80,128]{2,1,0:T(8,128)(2,1)S(1)} custom-call(s32[128,1,8]{2,1,0:T(1,128)S(1)} %all_to_all.20.asked, s32[1,64]{1,0:T(1,128)} %bitcast.9, s16[128,24,128]{2,1,0:T(8,128)(2,1)S(1)} %all_to_all.22.blocks), custom_call_target="tpu_custom_call" | custom-call | tf_op jit(solution)/shard_map/place/pallas_call | solution.py:229
  82.9 39.7 %all_to_all.23.code = s16[128,80,128]{2,1,0:T(8,128)(2,1)S(1)} all-to-all(s16[128,80,128]{2,1,0:T(8,128)(2,1)S(1)} %place.1), channel_id=1, replica_groups=mesh['gx'=8,'gy'=16] {'gx','gy'}, dimensions={0} | all-to-all | bytes 5242880 | tf_op jit(solution)/shard_map/all_to_all | solution.py:168
  122.6 2.7 %decode.1 = f32[128,24,384]{2,1,0:T(8,128)} custom-call(s16[128,80,128]{2,1,0:T(8,128)(2,1)S(1)} %all_to_all.23.code), custom_call_target="tpu_custom_call" | custom-call | tf_op jit(solution)/shard_map/decode/pallas_call | solution.py:241

commit v4 on v2

--- a/solution.py
+++ b/solution.py
@@ -26,37 +26,48 @@
     return jnp.ceil(8.0 * jnp.log2(jnp.maximum(top, TINY)))
 
 
-def gather_kernel(asked, prolong, out):
+def pick_kernel(asked, prolong, out, heads, held, named, sems):
+    load = pltpu.make_async_copy(prolong, held, sems.at[0])
+    load.start()
+    heads[...] = asked[...].T
+    name = pltpu.make_async_copy(heads, named, sems.at[1])
+    name.start()
+    name.wait()
+    load.wait()
+
     def step(d, carry):
-        out[d] = prolong[asked[d, 0, 0]]
+        out[d] = held[named[0, d]]
         return carry
 
     lax.fori_loop(0, out.shape[0], step, 0, unroll=16)
 
 
-def partial_kernel(slot, fetched, stiff, out, padded):
-    block = stiff.shape[0]
-    rows = fetched.shape[1]
-    first = pl.program_id(0) * block
+def partial_kernel(slot, fetched, far, out, padded, stiff, sems):
+    devices, rows, _ = fetched.shape
     per_row = stiff.shape[1]
-
-    @pl.when(pl.program_id(0) == 0)
-    def _():
-        def fill(t, carry):
-            padded[t, 0:rows, :] = fetched[t]
-            padded[t, rows:SUB, :] = jnp.zeros((SUB - rows, LANES), BF16)
-            return carry
-
-        lax.fori_loop(0, fetched.shape[0], fill, 0, unroll=8)
-
     lanes = lane_ids(rows)
-    for i in range(block):
-        t = first + i
+    parts = sems.shape[0]
+    block = devices // parts
+    copies = [
+        pltpu.make_async_copy(far.at[pl.ds(g * block, block)], stiff.at[pl.ds(g * block, block)], sems.at[g])
+        for g in range(parts)
+    ]
+    for copy in copies:
+        copy.start()
+
+    def fill(t, carry):
+        padded[t, 0:rows, :] = fetched[t]
+        padded[t, rows:SUB, :] = jnp.zeros((SUB - rows, LANES), BF16)
+        return carry
+
+    lax.fori_loop(0, devices, fill, 0, unroll=8)
+
+    def row(t):
         mine = padded[t]
         highs = []
         lows = []
         for q in range(0, per_row, 2):
-            pair = jnp.concatenate([stiff[i, q], stiff[i, q + 1]], axis=1)
+            pair = jnp.concatenate([stiff[t, q], stiff[t, q + 1]], axis=1)
             both = jnp.dot(mine, pair, preferred_element_type=F32)
             for h in range(2):
                 w = both[0:rows, h * LANES : (h + 1) * LANES]
@@ -75,10 +86,19 @@
         e = level(jnp.max(jnp.abs(value), axis=1, keepdims=True))
         code = jnp.round(value * (jnp.exp2(e * -0.125) * TOP))
         code = jnp.where(lanes == rows, e, code)
-        out[i] = code.astype(I16)
-
-
-def place_kernel(asked, owner, blocks, out, acc):
+        out[t] = code.astype(I16)
+
+    def step(g, carry):
+        rest = pl.ds(g * block, block)
+        pltpu.make_async_copy(far.at[rest], stiff.at[rest], sems.at[g]).wait()
+        for i in range(block):
+            row(g * block + i)
+        return carry
+
+    lax.fori_loop(0, parts, step, 0)
+
+
+def place_kernel(heads, owner, blocks, out, acc):
     devices, rows, _ = blocks.shape
     aggs = acc.shape[0]
     tiles = acc.shape[2] // LANES
@@ -103,19 +123,19 @@
         scale = jnp.exp2(code[:, rows : rows + 1] * 0.125) * (1.0 / TOP)
         sums = [jnp.zeros((rows, LANES), F32) for _ in range(tiles)]
         for q in range(4):
-            start = asked[d, 0, 1 + q]
+            start = heads[1 + q, d] * rows
             turned = pltpu.roll(code, (start - q * SUB + LANES) & (LANES - 1), 1)
             for m in range(tiles):
                 at = (lanes + m * LANES) - start
                 inside = at.astype(jnp.uint32) < rows
                 inside = jnp.concatenate([inside] * bands, axis=0)
                 sums[m] = jnp.where(inside, turned, sums[m])
-        a = asked[d, 0, 0]
+        a = heads[0, d]
         for m in range(tiles):
             acc[a, :, m * LANES : (m + 1) * LANES] += sums[m] * scale
         return carry
 
-    lax.fori_loop(0, devices, add, 0, unroll=8)
+    lax.fori_loop(0, devices, add, 0, unroll=32)
 
     def send(a, carry):
         parts = []
@@ -145,56 +165,72 @@
     return lax.all_to_all(x, AXES, split_axis=0, concat_axis=0, tiled=True)
 
 
+def in_hbm(x):
+    return pltpu.with_memory_space_constraint(x, pltpu.HBM)
+
+
+def grant(mib):
+    return pltpu.CompilerParams(vmem_limit_bytes=mib << 20)
+
+
 def per_device(prolong, stiffness, request, col_slot, col_pos, coarse_owner):
     devices = lax.axis_size(AXES)
     aggs, rows, dof = prolong.shape
     per_row = stiffness.shape[1]
     width = MAXNB * rows
     smem = pl.BlockSpec(memory_space=pltpu.SMEM)
-
-    asking = jnp.concatenate([request[:, None], col_pos * rows], axis=1)[:, None, :]
-    asked = swap(asking)
-
-    picked = pl.pallas_call(
-        gather_kernel,
-        out_shape=jax.ShapeDtypeStruct((devices, rows, dof), BF16),
-        in_specs=[smem, pl.BlockSpec(memory_space=pltpu.VMEM)],
-        out_specs=pl.BlockSpec(memory_space=pltpu.VMEM),
+    vmem = pl.BlockSpec(memory_space=pltpu.VMEM)
+    hbm = pl.BlockSpec(memory_space=pltpu.HBM)
+
+    asking = jnp.concatenate([request[:, None], col_pos, col_pos[:, 0:3]], axis=1)
+    asked = swap(asking[:, None, :])[:, 0, :]
+
+    picked, heads = pl.pallas_call(
+        pick_kernel,
+        out_shape=(
+            jax.ShapeDtypeStruct((devices, rows, dof), BF16),
+            jax.ShapeDtypeStruct((8, devices), I32),
+        ),
+        in_specs=[vmem, hbm],
+        out_specs=(vmem, vmem),
+        scratch_shapes=[
+            pltpu.VMEM((aggs, rows, dof), BF16),
+            pltpu.SMEM((8, devices), I32),
+            pltpu.SemaphoreType.DMA((2,)),
+        ],
+        compiler_params=grant(4),
         name="pick",
-        compiler_params=pltpu.CompilerParams(vmem_limit_bytes=4 << 20),
-    )(asked, prolong)
+    )(asked, in_hbm(prolong))
     fetched = swap(picked)
 
-    block = 32
     sent = pl.pallas_call(
         partial_kernel,
-        grid=(devices // block,),
         out_shape=jax.ShapeDtypeStruct((devices, rows, LANES), I16),
-        in_specs=[
-            smem,
-            pl.BlockSpec((devices, rows, dof), lambda g: (0, 0, 0)),
-            pl.BlockSpec((block, per_row, dof, dof), lambda g: (g, 0, 0, 0)),
+        in_specs=[smem, vmem, hbm],
+        out_specs=vmem,
+        scratch_shapes=[
+            pltpu.VMEM((devices, SUB, dof), BF16),
+            pltpu.VMEM((devices, per_row, dof, dof), BF16),
+            pltpu.SemaphoreType.DMA((4,)),
         ],
-        out_specs=pl.BlockSpec((block, rows, LANES), lambda g: (g, 0, 0)),
-        scratch_shapes=[pltpu.VMEM((devices, SUB, dof), BF16)],
+        compiler_params=grant(40),
         name="partial",
-        compiler_params=pltpu.CompilerParams(vmem_limit_bytes=48 << 20),
-    )(col_slot.T, fetched, stiffness)
+    )(in_hbm(col_slot.T), fetched, in_hbm(stiffness))
     blocks = swap(sent)
 
     depth = rows * (width // LANES) + 8
     rows_out = pl.pallas_call(
         place_kernel,
         out_shape=jax.ShapeDtypeStruct((devices, depth, LANES), I16),
-        in_specs=[smem, smem, pl.BlockSpec(memory_space=pltpu.VMEM)],
-        out_specs=pl.BlockSpec(memory_space=pltpu.VMEM),
+        in_specs=[smem, smem, vmem],
+        out_specs=vmem,
         scratch_shapes=[pltpu.VMEM((aggs, rows, width), F32)],
         name="place",
-        compiler_params=pltpu.CompilerParams(vmem_limit_bytes=16 << 20),
-    )(asked, coarse_owner.T, blocks)
+        compiler_params=grant(16),
+    )(heads, in_hbm(coarse_owner.T), blocks)
     arrived = swap(rows_out)
 
-    step = 16
+    step = 32
     return pl.pallas_call(
         decode_kernel,
         grid=(devices // step,),
@@ -202,7 +238,7 @@
         in_specs=[pl.BlockSpec((step, depth, LANES), lambda g: (g, 0, 0))],
         out_specs=pl.BlockSpec((step, rows, width), lambda g: (g, 0, 0)),
         name="decode",
-        compiler_params=pltpu.CompilerParams(vmem_limit_bytes=16 << 20),
+        compiler_params=grant(16),
     )(arrived)
 
 

time: 126 us -> 120 us (0.952)
  Pallas kernels: 21 us -> 17.2 us
  local copies, waits for them, and re-layouts: 1.8 us -> 0.1 us
    pallas_call x1, Pallas kernels: 6.33 us -> 4.57 us  [per_device(): pl.pallas_call(place_kernel, out_shape=jax.ShapeDtypeStruct((devices, dep...]
    unnamed x6 -> x0, local copies, waits for them, and re-layouts: 1.68 us -> none
where the time goes in v4:
time: 120 us; the launch traced here: 119 us
  blocking collectives  101 us (84%)
  Pallas kernels  17.2 us (14%)
    all_to_all x4, blocking collectives, swap(): return lax.all_to_all(x, AXES, split_axis=0, concat_axis=0, tiled=True)  101 us
    pallas_call x1, Pallas kernels, per_device(): pl.pallas_call(partial_kernel, out_shape=jax.ShapeDtypeStruct((devices, r...  8.71 us
    pallas_call x1, Pallas kernels, per_device(): pl.pallas_call(place_kernel, out_shape=jax.ShapeDtypeStruct((devices, dep...  4.57 us
    pallas_call x1, Pallas kernels, per_device(): pl.pallas_call(decode_kernel, grid=(devices // step,), out_shape=jax.Shap...  2.72 us

profile of v4, /device:TPU:1, one launch (start us, length us, event | category | flops | bytes accessed | tf_op | source)
XLA Modules:
  0.0 119.3 jit_solution(5865582155580563554)
XLA Ops:
  0.0 0.8 pad_add_fusion
  0.8 0.1 copy.10
  0.9 20.9 %all_to_all.20 = s32[128,1,8]{2,1,0:T(1,128)S(1)} all-to-all(s32[128,1,8]{2,1,0:T(1,128)S(1)} %bitcast.7), channel_id=1, replica_groups=mesh['gx'=8,'gy'=16] {'gx','gy'}, dimensions={0} | all-to-all | bytes 8192 | tf_op jit(solution)/shard_map/all_to_all | solution.py:165
  21.8 1.2 pick.1
  23.0 20.3 %all_to_all.21.fetched = bf16[128,24,128]{2,1,0:T(8,128)(2,1)S(1)} all-to-all(bf16[128,24,128]{2,1,0:T(8,128)(2,1)S(1)} %get-tuple-element.8), channel_id=1, replica_groups=mesh['gx'=8,'gy'=16] {'gx','gy'}, dimensions={0} | all-to-all | bytes 1572864 | tf_op jit(solution)/shard_map/all_to_all | solution.py:165
  43.3 8.7 %partial.1 = s16[128,24,128]{2,1,0:T(8,128)(2,1)S(1)} custom-call(s32[4,128]{1,0:T(4,128)} %bitcast.9, bf16[128,24,128]{2,1,0:T(8,128)(2,1)S(1)} %all_to_all.21.fetched, bf16[128,4,128,128]{3,2,1,0:T(8,128)(2,1)} %far.1), custom_call_target="tpu_custom_call" | custom-call | tf_op jit(solution)/shard_map/partial/pallas_call | solution.py:206
  52.0 20.4 %all_to_all.22.blocks = s16[128,24,128]{2,1,0:T(8,128)(2,1)S(1)} all-to-all(s16[128,24,128]{2,1,0:T(8,128)(2,1)S(1)} %partial.1), channel_id=1, replica_groups=mesh['gx'=8,'gy'=16] {'gx','gy'}, dimensions={0} | all-to-all | bytes 1572864 | tf_op jit(solution)/shard_map/all_to_all | solution.py:165
  72.3 4.6 %place.1 = s16[128,80,128]{2,1,0:T(8,128)(2,1)S(1)} custom-call(s32[8,128]{1,0:T(8,128)S(1)} %get-tuple-element.7.heads, s32[1,64]{1,0:T(1,128)} %bitcast.10, s16[128,24,128]{2,1,0:T(8,128)(2,1)S(1)} %all_to_all.22.blocks), custom_call_target="tpu_custom_call" | custom-call | tf_op jit(solution)/shard_map/place/pallas_call | solution.py:222
  76.9 39.7 %all_to_all.23.code = s16[128,80,128]{2,1,0:T(8,128)(2,1)S(1)} all-to-all(s16[128,80,128]{2,1,0:T(8,128)(2,1)S(1)} %place.1), channel_id=1, replica_groups=mesh['gx'=8,'gy'=16] {'gx','gy'}, dimensions={0} | all-to-all | bytes 5242880 | tf_op jit(solution)/shard_map/all_to_all | solution.py:165
  116.6 2.7 %decode.1 = f32[128,24,384]{2,1,0:T(8,128)} custom-call(s16[128,80,128]{2,1,0:T(8,128)(2,1)S(1)} %all_to_all.23.code), custom_call_target="tpu_custom_call" | custom-call | tf_op jit(solution)/shard_map/decode/pallas_call | solution.py:234

commit v5 on v4

--- a/solution.py
+++ b/solution.py
@@ -1,3 +1,6 @@
+import functools
+import math
+
 import jax
 import jax.numpy as jnp
 from jax import lax
@@ -13,13 +16,18 @@
 I32 = jnp.int32
 
 TOP = 32766.0
-TINY = 2.0**-120
+TINY = 2.0**-100
+FLOOR = 14
 LANES = 128
 SUB = 32
 
 
 def lane_ids(rows):
     return lax.broadcasted_iota(I32, (rows, LANES), 1)
+
+
+def codes(devices):
+    return TOP / (FLOOR + math.log2(devices))
 
 
 def level(top):
@@ -83,28 +91,37 @@
         value = prod[0:rows]
         for q in range(1, per_row):
             value = jnp.where(lanes < q * SUB, value, prod[q * rows : (q + 1) * rows])
-        e = level(jnp.max(jnp.abs(value), axis=1, keepdims=True))
+        top = jnp.max(jnp.abs(value), axis=1, keepdims=True)
+        e = level(top)
         code = jnp.round(value * (jnp.exp2(e * -0.125) * TOP))
         code = jnp.where(lanes == rows, e, code)
         out[t] = code.astype(I16)
-
-    def step(g, carry):
+        return top
+
+    def step(g, most):
         rest = pl.ds(g * block, block)
         pltpu.make_async_copy(far.at[rest], stiff.at[rest], sems.at[g]).wait()
         for i in range(block):
-            row(g * block + i)
-        return carry
-
-    lax.fori_loop(0, parts, step, 0)
-
-
-def place_kernel(heads, owner, blocks, out, acc):
+            most = jnp.maximum(most, row(g * block + i))
+        return most
+
+    most = lax.fori_loop(0, parts, step, jnp.zeros((rows, 1), F32))
+    most = jnp.broadcast_to(level(jnp.max(most, axis=0, keepdims=True)), (8, LANES)).astype(I16)
+    spare = lane_ids(8).astype(I16) == SUB + rows
+
+    def share(t, carry):
+        out[t, 0:8, :] = jnp.where(spare, most, out[t, 0:8, :])
+        return carry
+
+    lax.fori_loop(0, devices, share, 0, unroll=16)
+
+
+def place_kernel(heads, owner, blocks, out, unit, acc):
     devices, rows, _ = blocks.shape
     aggs = acc.shape[0]
     tiles = acc.shape[2] // LANES
     lanes = lane_ids(8)
     bands = rows // 8
-    sub8 = lax.broadcasted_iota(I32, (8, LANES), 0)
 
     def clear(a, carry):
         acc[a] = jnp.zeros(acc.shape[1:], F32)
@@ -118,7 +135,7 @@
 
     lax.fori_loop(0, devices, clear_out, 0, unroll=8)
 
-    def add(d, carry):
+    def add(d, most):
         code = blocks[d].astype(F32)
         scale = jnp.exp2(code[:, rows : rows + 1] * 0.125) * (1.0 / TOP)
         sums = [jnp.zeros((rows, LANES), F32) for _ in range(tiles)]
@@ -133,32 +150,36 @@
         a = heads[0, d]
         for m in range(tiles):
             acc[a, :, m * LANES : (m + 1) * LANES] += sums[m] * scale
-        return carry
-
-    lax.fori_loop(0, devices, add, 0, unroll=32)
+        return jnp.maximum(most, code[0:8])
+
+    most = lax.fori_loop(0, devices, add, jnp.full((8, LANES), -8.0 * 1024, F32), unroll=32)
+    most = jnp.broadcast_to(most[0:1, SUB + rows : SUB + rows + 1], (8, LANES))
+    unit[...] = most
+    inverse = jnp.exp2(FLOOR - most * 0.125)[0:1]
+    rate = codes(devices)
 
     def send(a, carry):
         parts = []
-        scales = jnp.zeros((8, LANES), F32)
         for m in range(tiles):
             value = acc[a, :, m * LANES : (m + 1) * LANES]
-            e = level(jnp.max(jnp.abs(value), axis=0, keepdims=True))
-            parts.append(jnp.round(value * (jnp.exp2(e * -0.125) * TOP)))
-            scales = jnp.where(sub8 == m, e, scales)
-        out[owner[0, a]] = jnp.concatenate(parts + [scales], axis=0).astype(I16)
+            size = jnp.log2(1.0 + jnp.abs(value) * inverse)
+            parts.append(jnp.round(size * jnp.where(value < 0.0, -rate, rate)))
+        out[owner[0, a]] = jnp.concatenate(parts, axis=0).astype(I16)
         return carry
 
     lax.fori_loop(0, aggs, send, 0, unroll=8)
 
 
-def decode_kernel(code, out):
+def decode_kernel(devices, unit, code, out):
     rows = out.shape[1]
     tiles = out.shape[2] // LANES
+    delta = jnp.exp2(unit[0:1] * 0.125 - FLOOR)
+    rate = 1.0 / codes(devices)
     for j in range(code.shape[0]):
-        x = code[j].astype(F32)
-        scales = jnp.exp2(x[rows * tiles : rows * tiles + 8] * 0.125) * (1.0 / TOP)
         for m in range(tiles):
-            out[j, :, m * LANES : (m + 1) * LANES] = x[rows * m : rows * (m + 1)] * scales[m : m + 1]
+            x = code[j, rows * m : rows * (m + 1)].astype(F32)
+            size = (jnp.exp2(jnp.abs(x) * rate) - 1.0) * jnp.where(x < 0.0, -delta, delta)
+            out[j, :, m * LANES : (m + 1) * LANES] = size
 
 
 def swap(x):
@@ -218,28 +239,34 @@
     )(in_hbm(col_slot.T), fetched, in_hbm(stiffness))
     blocks = swap(sent)
 
-    depth = rows * (width // LANES) + 8
-    rows_out = pl.pallas_call(
+    depth = rows * (width // LANES)
+    coarse, unit = pl.pallas_call(
         place_kernel,
-        out_shape=jax.ShapeDtypeStruct((devices, depth, LANES), I16),
+        out_shape=(
+            jax.ShapeDtypeStruct((devices, depth, LANES), I16),
+            jax.ShapeDtypeStruct((8, LANES), F32),
+        ),
         in_specs=[smem, smem, vmem],
-        out_specs=vmem,
+        out_specs=(vmem, vmem),
         scratch_shapes=[pltpu.VMEM((aggs, rows, width), F32)],
+        compiler_params=grant(16),
         name="place",
-        compiler_params=grant(16),
     )(heads, in_hbm(coarse_owner.T), blocks)
-    arrived = swap(rows_out)
+    arrived = swap(coarse)
 
     step = 32
     return pl.pallas_call(
-        decode_kernel,
+        functools.partial(decode_kernel, devices),
         grid=(devices // step,),
         out_shape=jax.ShapeDtypeStruct((devices, rows, width), F32),
-        in_specs=[pl.BlockSpec((step, depth, LANES), lambda g: (g, 0, 0))],
+        in_specs=[
+            pl.BlockSpec((8, LANES), lambda g: (0, 0)),
+            pl.BlockSpec((step, depth, LANES), lambda g: (g, 0, 0)),
+        ],
         out_specs=pl.BlockSpec((step, rows, width), lambda g: (g, 0, 0)),
+        compiler_params=grant(16),
         name="decode",
-        compiler_params=grant(16),
-    )(arrived)
+    )(unit, arrived)
 
 
 def solution(mesh):

time: 120 us -> 117 us (0.975)
  blocking collectives: 101 us -> 98.4 us
    all_to_all x4, blocking collectives: 101 us -> 98.4 us  [swap(): return lax.all_to_all(x, AXES, split_axis=0, concat_axis=0, tiled=True)]
where the time goes in v5:
time: 117 us
  blocking collectives  98.4 us (84%)
  Pallas kernels  17.6 us (15%)
    all_to_all x4, blocking collectives, swap(): return lax.all_to_all(x, AXES, split_axis=0, concat_axis=0, tiled=True)  98.4 us
    pallas_call x1, Pallas kernels, per_device(): pl.pallas_call(partial_kernel, out_shape=jax.ShapeDtypeStruct((devices, r...  8.79 us
    pallas_call x1, Pallas kernels, per_device(): pl.pallas_call(place_kernel, out_shape=(jax.ShapeDtypeStruct((devices, de...  4.54 us
    pallas_call x1, Pallas kernels, per_device(): pl.pallas_call(functools.partial(decode_kernel, devices), grid=(devices /...  3.12 us

profile of v5, /device:TPU:1, one launch (start us, length us, event | category | flops | bytes accessed | tf_op | source)
XLA Modules:
  0.0 117.0 jit_solution(9540159609702100973)
XLA Ops:
  0.0 0.8 pad_add_fusion
  0.8 0.1 copy.10
  0.9 20.9 %all_to_all.20 = s32[128,1,8]{2,1,0:T(1,128)S(1)} all-to-all(s32[128,1,8]{2,1,0:T(1,128)S(1)} %bitcast.7), channel_id=1, replica_groups=mesh['gx'=8,'gy'=16] {'gx','gy'}, dimensions={0} | all-to-all | bytes 8192 | tf_op jit(solution)/shard_map/all_to_all | solution.py:186
  21.8 1.2 %pick.1 = (bf16[128,24,128]{2,1,0:T(8,128)(2,1)S(1)}, s32[8,128]{1,0:T(8,128)S(1)}) custom-call(s32[128,8]{1,0:T(8,128)S(1)} %bitcast.6, bf16[64,24,128]{2,1,0:T(8,128)(2,1)} %prolong.1), custom_call_target="tpu_custom_call" | custom-call | tf_op jit(solution)/shard_map/pick/pallas_call | solution.py:209
  23.0 20.3 %all_to_all.21.fetched = bf16[128,24,128]{2,1,0:T(8,128)(2,1)S(1)} all-to-all(bf16[128,24,128]{2,1,0:T(8,128)(2,1)S(1)} %get-tuple-element.10), channel_id=1, replica_groups=mesh['gx'=8,'gy'=16] {'gx','gy'}, dimensions={0} | all-to-all | bytes 1572864 | tf_op jit(solution)/shard_map/all_to_all | solution.py:186
  43.3 8.8 %partial.1 = s16[128,24,128]{2,1,0:T(8,128)(2,1)S(1)} custom-call(s32[4,128]{1,0:T(4,128)} %bitcast.9, bf16[128,24,128]{2,1,0:T(8,128)(2,1)S(1)} %all_to_all.21.fetched, bf16[128,4,128,128]{3,2,1,0:T(8,128)(2,1)} %far.1), custom_call_target="tpu_custom_call" | custom-call | tf_op jit(solution)/shard_map/partial/pallas_call | solution.py:227
  52.1 20.3 %all_to_all.22.blocks = s16[128,24,128]{2,1,0:T(8,128)(2,1)S(1)} all-to-all(s16[128,24,128]{2,1,0:T(8,128)(2,1)S(1)} %partial.1), channel_id=1, replica_groups=mesh['gx'=8,'gy'=16] {'gx','gy'}, dimensions={0} | all-to-all | bytes 1572864 | tf_op jit(solution)/shard_map/all_to_all | solution.py:186
  72.4 4.5 %place.1 = (s16[128,72,128]{2,1,0:T(8,128)(2,1)S(1)}, f32[8,128]{1,0:T(8,128)S(1)}) custom-call(s32[8,128]{1,0:T(8,128)S(1)} %get-tuple-element.9.heads, s32[1,64]{1,0:T(1,128)} %bitcast.11, s16[128,24,128]{2,1,0:T(8,128)(2,1)S(1)} %all_to_all.22.blocks), custom_call_target="tpu_custom_call" | custom-call | tf_op jit(solution)/shard_map/place/pallas_call | solution.py:243
  76.9 36.9 %all_to_all.23.code = s16[128,72,128]{2,1,0:T(8,128)(2,1)S(1)} all-to-all(s16[128,72,128]{2,1,0:T(8,128)(2,1)S(1)} %get-tuple-element.12), channel_id=1, replica_groups=mesh['gx'=8,'gy'=16] {'gx','gy'}, dimensions={0} | all-to-all | bytes 4718592 | tf_op jit(solution)/shard_map/all_to_all | solution.py:186
  113.8 3.1 %decode.1 = f32[128,24,384]{2,1,0:T(8,128)} custom-call(f32[8,128]{1,0:T(8,128)S(1)} %get-tuple-element.11.unit, s16[128,72,128]{2,1,0:T(8,128)(2,1)S(1)} %all_to_all.23.code), custom_call_target="tpu_custom_call" | custom-call | tf_op jit(solution)/shard_map/decode/pallas_call | solution.py:258

commit v6 on v5

v6 whole, which is shorter than its diff:
```python
import math

import jax
import jax.numpy as jnp
from jax import lax
from jax.experimental import pallas as pl
from jax.experimental.pallas import tpu as pltpu
from jax.sharding import PartitionSpec as P

MAXNB = 16
AXES = ("gx", "gy")
F32 = jnp.float32
BF16 = jnp.bfloat16
I16 = jnp.int16
I32 = jnp.int32

TOP = 32766.0
TINY = 2.0**-100
FLOOR = 14
DEPTH = 4
LANES = 128
SUB = 32


def lane_ids(rows):
    return lax.broadcasted_iota(I32, (rows, LANES), 1)


def codes(devices):
    return TOP / (FLOOR + math.log2(devices))


def level(top):
    return jnp.ceil(8.0 * jnp.log2(jnp.maximum(top, TINY)))


def pick_kernel(asked, prolong, far, out, heads, near, held, named, sems):
    load = pltpu.make_async_copy(prolong, held, sems.at[0])
    load.start()
    ways = sems.shape[0] - 2
    size = near.shape[0] // ways
    ahead = [
        pltpu.make_async_copy(far.at[pl.ds(w * size, size)], near.at[pl.ds(w * size, size)], sems.at[2 + w])
        for w in range(ways)
    ]
    for copy in ahead:
        copy.start()
    heads[...] = asked[...].T
    name = pltpu.make_async_copy(heads, named, sems.at[1])
    name.start()
    name.wait()
    load.wait()

    def step(d, carry):
        out[d] = held[named[0, d]]
        return carry

    lax.fori_loop(0, out.shape[0], step, 0, unroll=16)
    for copy in ahead:
        copy.wait()


def partial_kernel(slot, fetched, near, far, out, padded, pairs, stiff, sems):
    devices, rows, dof = fetched.shape
    per_row = stiff.shape[1]
    lanes = lane_ids(rows)
    parts = sems.shape[0]
    block = near.shape[0]
    copies = [
        pltpu.make_async_copy(far.at[pl.ds((g + 1) * block, block)], stiff.at[pl.ds(g * block, block)], sems.at[g])
        for g in range(parts)
    ]
    for copy in copies:
        copy.start()

    def fill(p, carry):
        pairs[p] = jnp.zeros(pairs.shape[1:], BF16)
        for h in range(2):
            mine = fetched[2 * p + h]
            padded[2 * p + h, 0:rows, :] = mine
            padded[2 * p + h, rows:SUB, :] = jnp.zeros((SUB - rows, LANES), BF16)
            pairs[p, SUB * h : SUB * h + rows, LANES * h : LANES * (h + 1)] = mine
        return carry

    lax.fori_loop(0, devices // 2, fill, 0, unroll=4)

    def products(*accs):
        most = jnp.zeros((rows, 1), F32)

        def first(p):
            held, t = (near, 2 * p) if 2 * p < block else (stiff, 2 * p - block)
            for c in range(2):
                tile = jnp.concatenate(
                    [
                        jnp.concatenate([held[t + h, 2 * c], held[t + h, 2 * c + 1]], axis=1)
                        for h in range(2)
                    ],
                    axis=0,
                )
                pltpu.matmul_push_rhs(tile, staging_register=c, mxu_index=0)
                pltpu.matmul_acc_lhs(accs[2 * (p % DEPTH) + c], pairs[p], load_staged_rhs=c)

        def second(p):
            both = [pltpu.matmul_pop(accs[2 * (p % DEPTH) + c]) for c in range(2)]
            lefts = []
            rights = []
            for h in range(2):
                highs = []
                lows = []
                for q in range(per_row):
                    w = both[q // 2][SUB * h : SUB * h + rows, (q % 2) * LANES : (q % 2 + 1) * LANES]
                    high = w.astype(BF16).astype(F32)
                    highs.append(high)
                    lows.append(w - high)
                lefts.append(
                    jnp.concatenate(
                        [jnp.concatenate(highs, axis=0).astype(BF16), jnp.concatenate(lows, axis=0).astype(BF16)],
                        axis=1,
                    )
                )
                rights += [padded[slot[q, 2 * p + h]] for q in range(per_row)]
            right = jnp.concatenate(rights, axis=0)
            right = jnp.concatenate([right, right], axis=1)
            pltpu.matmul_push_rhs(right, staging_register=p % 2, mxu_index=1, transpose=True)
            pltpu.matmul_acc_lhs(accs[2 * DEPTH + p % DEPTH], jnp.concatenate(lefts, axis=0), load_staged_rhs=p % 2)

        def third(p, most):
            prod = pltpu.matmul_pop(accs[2 * DEPTH + p % DEPTH])
            for h in range(2):
                mine = prod[h * per_row * rows : (h + 1) * per_row * rows, h * LANES : (h + 1) * LANES]
                value = mine[0:rows]
                for q in range(1, per_row):
                    value = jnp.where(lanes < q * SUB, value, mine[q * rows : (q + 1) * rows])
                top = jnp.max(jnp.abs(value), axis=1, keepdims=True)
                most = jnp.maximum(most, top)
                e = level(top)
                code = jnp.round(value * (jnp.exp2(e * -0.125) * TOP))
                code = jnp.where(lanes == rows, e, code)
                out[2 * p + h] = code.astype(I16)
            return most

        count = devices // 2
        for i in range(count + 2 * (DEPTH - 1)):
            if 0 < i < count and (2 * i) % block == 0:
                copies[2 * i // block - 1].wait()
            if i < count:
                first(i)
            if 0 <= i - (DEPTH - 1) < count:
                second(i - (DEPTH - 1))
            if 0 <= i - 2 * (DEPTH - 1) < count:
                most = third(i - 2 * (DEPTH - 1), most)

        most = jnp.broadcast_to(level(jnp.max(most, axis=0, keepdims=True)), (8, LANES)).astype(I16)
        spare = lane_ids(8).astype(I16) == SUB + rows

        def share(t, carry):
            out[t, 0:8, :] = jnp.where(spare, most, out[t, 0:8, :])
            return carry

        lax.fori_loop(0, devices, share, 0, unroll=16)

    wide = 2 * LANES
    pl.run_scoped(
        products,
        *[pltpu.ACC(0)((2 * SUB, wide), F32) for _ in range(2 * DEPTH)],
        *[pltpu.ACC(1)((2 * per_row * rows, wide), F32) for _ in range(DEPTH)],
    )


def place_kernel(heads, owner, blocks, out, unit, acc):
    devices, rows, _ = blocks.shape
    aggs = acc.shape[0]
    tiles = acc.shape[2] // LANES
    lanes = lane_ids(8)
    bands = rows // 8

    def clear(a, carry):
        acc[a] = jnp.zeros(acc.shape[1:], F32)
        return carry

    lax.fori_loop(0, aggs, clear, 0, unroll=8)

    def clear_out(d, carry):
        out[d] = jnp.zeros(out.shape[1:], I16)
        return carry

    lax.fori_loop(0, devices, clear_out, 0, unroll=8)

    def add(d, most):
        code = blocks[d].astype(F32)
        scale = jnp.exp2(code[:, rows : rows + 1] * 0.125) * (1.0 / TOP)
        sums = [jnp.zeros((rows, LANES), F32) for _ in range(tiles)]
        for q in range(4):
            start = heads[1 + q, d] * rows
            turned = pltpu.roll(code, (start - q * SUB + LANES) & (LANES - 1), 1)
            for m in range(tiles):
                at = (lanes + m * LANES) - start
                inside = at.astype(jnp.uint32) < rows
                inside = jnp.concatenate([inside] * bands, axis=0)
                sums[m] = jnp.where(inside, turned, sums[m])
        a = heads[0, d]
        for m in range(tiles):
            acc[a, :, m * LANES : (m + 1) * LANES] += sums[m] * scale
        return jnp.maximum(most, code[0:8])

    most = lax.fori_loop(0, devices, add, jnp.full((8, LANES), -8.0 * 1024, F32), unroll=32)
    most = jnp.broadcast_to(most[0:1, SUB + rows : SUB + rows + 1], (8, LANES))
    unit[...] = most
    inverse = jnp.exp2(FLOOR - most * 0.125)[0:1]
    rate = codes(devices)

    def send(a, carry):
        parts = []
        for m in range(tiles):
            value = acc[a, :, m * LANES : (m + 1) * LANES]
            size = jnp.log2(1.0 + jnp.abs(value) * inverse)
            parts.append(jnp.round(size * jnp.where(value < 0.0, -rate, rate)))
        out[owner[0, a]] = jnp.concatenate(parts, axis=0).astype(I16)
        return carry

    lax.fori_loop(0, aggs, send, 0, unroll=8)


def decode_kernel(unit, code, out, ready, sems):
    devices, rows, width = ready.shape
    parts = sems.shape[0]
    block = devices // parts
    delta = jnp.exp2(unit[0:1] * 0.125 - FLOOR)
    rate = 1.0 / codes(devices)

    def copy(g):
        here = pl.ds(g * block, block)
        return pltpu.make_async_copy(ready.at[here], out.at[here], sems.at[g])

    def step(g, carry):
        for j in range(block):
            d = g * block + j
            for m in range(width // LANES):
                x = code[d, rows * m : rows * (m + 1)].astype(F32)
                size = (jnp.exp2(jnp.abs(x) * rate) - 1.0) * jnp.where(x < 0.0, -delta, delta)
                ready[d, :, m * LANES : (m + 1) * LANES] = size
        copy(g).start()
        return carry

    lax.fori_loop(0, parts, step, 0)

    def finish(g, carry):
        copy(g).wait()
        return carry

    lax.fori_loop(0, parts, finish, 0)


def swap(x):
    return lax.all_to_all(x, AXES, split_axis=0, concat_axis=0, tiled=True)


def in_hbm(x):
    return pltpu.with_memory_space_constraint(x, pltpu.HBM)


def grant(mib):
    return pltpu.CompilerParams(vmem_limit_bytes=mib << 20)


def per_device(prolong, stiffness, request, col_slot, col_pos, coarse_owner):
    devices = lax.axis_size(AXES)
    aggs, rows, dof = prolong.shape
    per_row = stiffness.shape[1]
    width = MAXNB * rows
    smem = pl.BlockSpec(memory_space=pltpu.SMEM)
    vmem = pl.BlockSpec(memory_space=pltpu.VMEM)
    hbm = pl.BlockSpec(memory_space=pltpu.HBM)

    asking = jnp.concatenate([request[:, None], col_pos, col_pos[:, 0:3]], axis=1)
    asked = swap(asking[:, None, :])[:, 0, :]

    block = devices // 8
    picked, heads, near = pl.pallas_call(
        pick_kernel,
        out_shape=(
            jax.ShapeDtypeStruct((devices, rows, dof), BF16),
            jax.ShapeDtypeStruct((8, devices), I32),
            jax.ShapeDtypeStruct((block, per_row, dof, dof), BF16),
        ),
        in_specs=[vmem, hbm, hbm],
        out_specs=(vmem, vmem, vmem),
        scratch_shapes=[
            pltpu.VMEM((aggs, rows, dof), BF16),
            pltpu.SMEM((8, devices), I32),
            pltpu.SemaphoreType.DMA((6,)),
        ],
        compiler_params=grant(8),
        name="pick",
    )(asked, in_hbm(prolong), in_hbm(stiffness))
    fetched = swap(picked)

    sent = pl.pallas_call(
        partial_kernel,
        out_shape=jax.ShapeDtypeStruct((devices, rows, LANES), I16),
        in_specs=[smem, vmem, vmem, hbm],
        out_specs=vmem,
        scratch_shapes=[
            pltpu.VMEM((devices, SUB, dof), BF16),
            pltpu.VMEM((devices // 2, 2 * SUB, 2 * dof), BF16),
            pltpu.VMEM((devices - block, per_row, dof, dof), BF16),
            pltpu.SemaphoreType.DMA((devices // block - 1,)),
        ],
        compiler_params=grant(40),
        name="partial",
    )(in_hbm(col_slot.T), fetched, near, in_hbm(stiffness))
    blocks = swap(sent)

    depth = rows * (width // LANES)
    coarse, unit = pl.pallas_call(
        place_kernel,
        out_shape=(
            jax.ShapeDtypeStruct((devices, depth, LANES), I16),
            jax.ShapeDtypeStruct((8, LANES), F32),
        ),
        in_specs=[smem, smem, vmem],
        out_specs=(vmem, vmem),
        scratch_shapes=[pltpu.VMEM((aggs, rows, width), F32)],
        compiler_params=grant(16),
        name="place",
    )(heads, in_hbm(coarse_owner.T), blocks)
    arrived = swap(coarse)

    return pl.pallas_call(
        decode_kernel,
        out_shape=jax.ShapeDtypeStruct((devices, rows, width), F32),
        in_specs=[vmem, vmem],
        out_specs=hbm,
        scratch_shapes=[pltpu.VMEM((devices, rows, width), F32), pltpu.SemaphoreType.DMA((4,))],
        compiler_params=grant(16),
        name="decode",
    )(unit, arrived)


def solution(mesh):
    placed = (
        P(AXES, None, None),
        P(AXES, None, None, None),
        P(AXES),
        P(AXES, None),
        P(AXES, None),
        P(AXES, None),
    )
    return jax.shard_map(
        per_device, mesh=mesh, in_specs=placed, out_specs=P(AXES, None, None), check_vma=False
    )
```

time: 117 us -> 116 us (level)
  no operation moved by 1% of the time
where the time goes in v6:
time: 116 us
  blocking collectives  98.4 us (85%)
  Pallas kernels  16.5 us (14%)
    all_to_all x4, blocking collectives, swap(): return lax.all_to_all(x, AXES, split_axis=0, concat_axis=0, tiled=True)  98.4 us
    pallas_call x1, Pallas kernels, per_device(): pl.pallas_call(partial_kernel, out_shape=jax.ShapeDtypeStruct((devices, r...  7.69 us
    pallas_call x1, Pallas kernels, per_device(): pl.pallas_call(place_kernel, out_shape=(jax.ShapeDtypeStruct((devices, de...  4.54 us
    pallas_call x1, Pallas kernels, per_device(): pl.pallas_call(decode_kernel, out_shape=jax.ShapeDtypeStruct((devices, ro...  2.57 us

profile of v6, /device:TPU:1, one launch (start us, length us, event | category | flops | bytes accessed | tf_op | source)
XLA Modules:
  0.0 115.8 jit_solution(9275492215305423500)
XLA Ops:
  0.0 0.8 pad_add_fusion
  0.8 0.1 copy.10
  0.9 20.9 %all_to_all.20 = s32[128,1,8]{2,1,0:T(1,128)S(1)} all-to-all(s32[128,1,8]{2,1,0:T(1,128)S(1)} %bitcast.7), channel_id=1, replica_groups=mesh['gx'=8,'gy'=16] {'gx','gy'}, dimensions={0} | all-to-all | bytes 8192 | tf_op jit(solution)/shard_map/all_to_all | solution.py:255
  21.8 1.7 %pick.1 = (bf16[128,24,128]{2,1,0:T(8,128)(2,1)S(1)}, s32[8,128]{1,0:T(8,128)S(1)}, bf16[16,4,128,128]{3,2,1,0:T(8,128)(2,1)S(1)}) custom-call(s32[128,8]{1,0:T(8,128)S(1)} %bitcast.6, bf16[64,24,128]{2,1,0:T(8,128)(2,1)} %prolong.1, bf16[128,4,128,128]{3,2,1,0:T(8,128)(2,1)} %far.3), custom_call_target="tpu_custom_call" | custom-call | tf_op jit(solution)/shard_map/pick/pallas_call | solution.py:279
  23.5 20.3 %all_to_all.21.fetched = bf16[128,24,128]{2,1,0:T(8,128)(2,1)S(1)} all-to-all(bf16[128,24,128]{2,1,0:T(8,128)(2,1)S(1)} %get-tuple-element.11), channel_id=1, replica_groups=mesh['gx'=8,'gy'=16] {'gx','gy'}, dimensions={0} | all-to-all | bytes 1572864 | tf_op jit(solution)/shard_map/all_to_all | solution.py:255
  43.8 7.7 %partial.1 = s16[128,24,128]{2,1,0:T(8,128)(2,1)S(1)} custom-call(s32[4,128]{1,0:T(4,128)} %bitcast.9, bf16[128,24,128]{2,1,0:T(8,128)(2,1)S(1)} %all_to_all.21.fetched, bf16[16,4,128,128]{3,2,1,0:T(8,128)(2,1)S(1)} %get-tuple-element.12.near, bf16[128,4,128,128]{3,2,1,0:T(8,128)(2,1)} %far.3), custom_call_target="tpu_custom_call" | custom-call | tf_op jit(solution)/shard_map/partial/pallas_call | solution.py:298
  51.5 20.4 %all_to_all.22.blocks = s16[128,24,128]{2,1,0:T(8,128)(2,1)S(1)} all-to-all(s16[128,24,128]{2,1,0:T(8,128)(2,1)S(1)} %partial.1), channel_id=1, replica_groups=mesh['gx'=8,'gy'=16] {'gx','gy'}, dimensions={0} | all-to-all | bytes 1572864 | tf_op jit(solution)/shard_map/all_to_all | solution.py:255
  71.8 4.5 %place.1 = (s16[128,72,128]{2,1,0:T(8,128)(2,1)S(1)}, f32[8,128]{1,0:T(8,128)S(1)}) custom-call(s32[8,128]{1,0:T(8,128)S(1)} %get-tuple-element.10.heads, s32[1,64]{1,0:T(1,128)} %bitcast.11, s16[128,24,128]{2,1,0:T(8,128)(2,1)S(1)} %all_to_all.22.blocks), custom_call_target="tpu_custom_call" | custom-call | tf_op jit(solution)/shard_map/place/pallas_call | solution.py:315
  76.4 36.9 %all_to_all.23.code = s16[128,72,128]{2,1,0:T(8,128)(2,1)S(1)} all-to-all(s16[128,72,128]{2,1,0:T(8,128)(2,1)S(1)} %get-tuple-element.14), channel_id=1, replica_groups=mesh['gx'=8,'gy'=16] {'gx','gy'}, dimensions={0} | all-to-all | bytes 4718592 | tf_op jit(solution)/shard_map/all_to_all | solution.py:255
  113.2 2.6 %decode.1 = f32[128,24,384]{2,1,0:T(8,128)} custom-call(f32[8,128]{1,0:T(8,128)S(1)} %get-tuple-element.13.unit, s16[128,72,128]{2,1,0:T(8,128)(2,1)S(1)} %all_to_all.23.code), custom_call_target="tpu_custom_call" | custom-call | tf_op jit(solution)/shard_map/decode/pallas_call | solution.py:329

commit v7 on v6

--- a/solution.py
+++ b/solution.py
@@ -34,17 +34,9 @@
     return jnp.ceil(8.0 * jnp.log2(jnp.maximum(top, TINY)))
 
 
-def pick_kernel(asked, prolong, far, out, heads, near, held, named, sems):
+def pick_kernel(asked, prolong, stiff, slot, owner, out, heads, held, named, sems):
     load = pltpu.make_async_copy(prolong, held, sems.at[0])
     load.start()
-    ways = sems.shape[0] - 2
-    size = near.shape[0] // ways
-    ahead = [
-        pltpu.make_async_copy(far.at[pl.ds(w * size, size)], near.at[pl.ds(w * size, size)], sems.at[2 + w])
-        for w in range(ways)
-    ]
-    for copy in ahead:
-        copy.start()
     heads[...] = asked[...].T
     name = pltpu.make_async_copy(heads, named, sems.at[1])
     name.start()
@@ -56,23 +48,12 @@
         return carry
 
     lax.fori_loop(0, out.shape[0], step, 0, unroll=16)
-    for copy in ahead:
-        copy.wait()
-
-
-def partial_kernel(slot, fetched, near, far, out, padded, pairs, stiff, sems):
+
+
+def partial_kernel(slot, fetched, stiff, out, padded, pairs):
     devices, rows, dof = fetched.shape
     per_row = stiff.shape[1]
     lanes = lane_ids(rows)
-    parts = sems.shape[0]
-    block = near.shape[0]
-    copies = [
-        pltpu.make_async_copy(far.at[pl.ds((g + 1) * block, block)], stiff.at[pl.ds(g * block, block)], sems.at[g])
-        for g in range(parts)
-    ]
-    for copy in copies:
-        copy.start()
-
     def fill(p, carry):
         pairs[p] = jnp.zeros(pairs.shape[1:], BF16)
         for h in range(2):
@@ -88,11 +69,10 @@
         most = jnp.zeros((rows, 1), F32)
 
         def first(p):
-            held, t = (near, 2 * p) if 2 * p < block else (stiff, 2 * p - block)
             for c in range(2):
                 tile = jnp.concatenate(
                     [
-                        jnp.concatenate([held[t + h, 2 * c], held[t + h, 2 * c + 1]], axis=1)
+                        jnp.concatenate([stiff[2 * p + h, 2 * c], stiff[2 * p + h, 2 * c + 1]], axis=1)
                         for h in range(2)
                     ],
                     axis=0,
@@ -141,8 +121,6 @@
 
         count = devices // 2
         for i in range(count + 2 * (DEPTH - 1)):
-            if 0 < i < count and (2 * i) % block == 0:
-                copies[2 * i // block - 1].wait()
             if i < count:
                 first(i)
             if 0 <= i - (DEPTH - 1) < count:
@@ -259,6 +237,10 @@
     return pltpu.with_memory_space_constraint(x, pltpu.HBM)
 
 
+def on_chip(x):
+    return pltpu.with_memory_space_constraint(x, pltpu.VMEM)
+
+
 def grant(mib):
     return pltpu.CompilerParams(vmem_limit_bytes=mib << 20)
 
@@ -275,40 +257,36 @@
     asking = jnp.concatenate([request[:, None], col_pos, col_pos[:, 0:3]], axis=1)
     asked = swap(asking[:, None, :])[:, 0, :]
 
-    block = devices // 8
-    picked, heads, near = pl.pallas_call(
+    picked, heads = pl.pallas_call(
         pick_kernel,
         out_shape=(
             jax.ShapeDtypeStruct((devices, rows, dof), BF16),
             jax.ShapeDtypeStruct((8, devices), I32),
-            jax.ShapeDtypeStruct((block, per_row, dof, dof), BF16),
         ),
-        in_specs=[vmem, hbm, hbm],
-        out_specs=(vmem, vmem, vmem),
+        in_specs=[vmem, hbm, hbm, hbm, hbm],
+        out_specs=(vmem, vmem),
         scratch_shapes=[
             pltpu.VMEM((aggs, rows, dof), BF16),
             pltpu.SMEM((8, devices), I32),
-            pltpu.SemaphoreType.DMA((6,)),
+            pltpu.SemaphoreType.DMA((2,)),
         ],
-        compiler_params=grant(8),
+        compiler_params=grant(4),
         name="pick",
-    )(asked, in_hbm(prolong), in_hbm(stiffness))
+    )(asked, in_hbm(prolong), in_hbm(stiffness), in_hbm(col_slot.T), in_hbm(coarse_owner.T))
     fetched = swap(picked)
 
     sent = pl.pallas_call(
         partial_kernel,
         out_shape=jax.ShapeDtypeStruct((devices, rows, LANES), I16),
-        in_specs=[smem, vmem, vmem, hbm],
+        in_specs=[smem, vmem, vmem],
         out_specs=vmem,
         scratch_shapes=[
             pltpu.VMEM((devices, SUB, dof), BF16),
             pltpu.VMEM((devices // 2, 2 * SUB, 2 * dof), BF16),
-            pltpu.VMEM((devices - block, per_row, dof, dof), BF16),
-            pltpu.SemaphoreType.DMA((devices // block - 1,)),
         ],
-        compiler_params=grant(40),
+        compiler_params=grant(16),
         name="partial",
-    )(in_hbm(col_slot.T), fetched, near, in_hbm(stiffness))
+    )(on_chip(col_slot.T), fetched, on_chip(stiffness))
     blocks = swap(sent)
 
     depth = rows * (width // LANES)
@@ -323,7 +301,7 @@
         scratch_shapes=[pltpu.VMEM((aggs, rows, width), F32)],
         compiler_params=grant(16),
         name="place",
-    )(heads, in_hbm(coarse_owner.T), blocks)
+    )(heads, on_chip(coarse_owner.T), blocks)
     arrived = swap(coarse)
 
     return pl.pallas_call(

time: 116 us -> 114 us (0.983)
  Pallas kernels: 16.5 us -> 14.4 us
    pallas_call x1, Pallas kernels: 7.69 us -> 6.11 us  [per_device(): pl.pallas_call(partial_kernel, out_shape=jax.ShapeDtypeStruct((devices, r...]
where the time goes in v7:
time: 114 us
  blocking collectives  98.4 us (86%)
  Pallas kernels  14.4 us (13%)
    all_to_all x4, blocking collectives, swap(): return lax.all_to_all(x, AXES, split_axis=0, concat_axis=0, tiled=True)  98.4 us
    pallas_call x1, Pallas kernels, per_device(): pl.pallas_call(partial_kernel, out_shape=jax.ShapeDtypeStruct((devices, r...  6.11 us
    pallas_call x1, Pallas kernels, per_device(): pl.pallas_call(place_kernel, out_shape=(jax.ShapeDtypeStruct((devices, de...  4.41 us
    pallas_call x1, Pallas kernels, per_device(): pl.pallas_call(decode_kernel, out_shape=jax.ShapeDtypeStruct((devices, ro...  2.57 us

profile of v7, /device:TPU:1, one launch (start us, length us, event | category | flops | bytes accessed | tf_op | source)
XLA Modules:
  0.0 113.8 jit_solution(17789077999771843341)
XLA Ops:
  0.0 0.8 pad_add_fusion
  0.8 0.1 copy.10
  0.9 20.9 %all_to_all.20 = s32[128,1,8]{2,1,0:T(1,128)S(1)} all-to-all(s32[128,1,8]{2,1,0:T(1,128)S(1)} %bitcast.11), channel_id=1, replica_groups=mesh['gx'=8,'gy'=16] {'gx','gy'}, dimensions={0} | all-to-all | bytes 8192 | tf_op jit(solution)/shard_map/all_to_all | solution.py:233
  21.8 0.0 copy-start
  21.8 0.0 copy-start.1
  21.8 1.3 %pick.1 = (bf16[128,24,128]{2,1,0:T(8,128)(2,1)S(1)}, s32[8,128]{1,0:T(8,128)S(1)}) custom-call(s32[128,8]{1,0:T(8,128)S(1)} %bitcast.6, bf16[64,24,128]{2,1,0:T(8,128)(2,1)} %prolong.1, bf16[128,4,128,128]{3,2,1,0:T(8,128)(2,1)} %stiff.3, s32[4,128]{1,0:T(4,128)} %bitcast.7, s32[1,64]{1,0:T(1,128)} %bitcast.9), custom_call_target="tpu_custom_call" | custom-call | tf_op jit(solution)/shard_map/pick/pallas_call | solution.py:260
  23.1 20.3 %all_to_all.21.fetched = bf16[128,24,128]{2,1,0:T(8,128)(2,1)S(1)} all-to-all(bf16[128,24,128]{2,1,0:T(8,128)(2,1)S(1)} %get-tuple-element.10), channel_id=1, replica_groups=mesh['gx'=8,'gy'=16] {'gx','gy'}, dimensions={0} | all-to-all | bytes 1572864 | tf_op jit(solution)/shard_map/all_to_all | solution.py:233
  43.4 0.0 copy-done
  43.4 0.0 copy-done.1
  43.4 0.0 copy-start.2
  43.4 6.1 %partial.1 = s16[128,24,128]{2,1,0:T(8,128)(2,1)S(1)} custom-call(s32[4,128]{1,0:T(4,128)S(1)} %bitcast.8, bf16[128,24,128]{2,1,0:T(8,128)(2,1)S(1)} %all_to_all.21.fetched, bf16[128,4,128,128]{3,2,1,0:T(8,128)(2,1)S(1)} %copy-done), custom_call_target="tpu_custom_call" | custom-call | tf_op jit(solution)/shard_map/partial/pallas_call | solution.py:278
  49.5 20.3 %all_to_all.22.blocks = s16[128,24,128]{2,1,0:T(8,128)(2,1)S(1)} all-to-all(s16[128,24,128]{2,1,0:T(8,128)(2,1)S(1)} %partial.1), channel_id=1, replica_groups=mesh['gx'=8,'gy'=16] {'gx','gy'}, dimensions={0} | all-to-all | bytes 1572864 | tf_op jit(solution)/shard_map/all_to_all | solution.py:233
  69.9 0.0 copy-done.2
  69.9 4.4 %place.1 = (s16[128,72,128]{2,1,0:T(8,128)(2,1)S(1)}, f32[8,128]{1,0:T(8,128)S(1)}) custom-call(s32[8,128]{1,0:T(8,128)S(1)} %get-tuple-element.9.heads, s32[1,64]{1,0:T(1,128)S(1)} %bitcast.10, s16[128,24,128]{2,1,0:T(8,128)(2,1)S(1)} %all_to_all.22.blocks), custom_call_target="tpu_custom_call" | custom-call | tf_op jit(solution)/shard_map/place/pallas_call | solution.py:293
  74.3 36.9 %all_to_all.23.code = s16[128,72,128]{2,1,0:T(8,128)(2,1)S(1)} all-to-all(s16[128,72,128]{2,1,0:T(8,128)(2,1)S(1)} %get-tuple-element.12), channel_id=1, replica_groups=mesh['gx'=8,'gy'=16] {'gx','gy'}, dimensions={0} | all-to-all | bytes 4718592 | tf_op jit(solution)/shard_map/all_to_all | solution.py:233
  111.2 2.6 %decode.1 = f32[128,24,384]{2,1,0:T(8,128)} custom-call(f32[8,128]{1,0:T(8,128)S(1)} %get-tuple-element.11.unit, s16[128,72,128]{2,1,0:T(8,128)(2,1)S(1)} %all_to_all.23.code), custom_call_target="tpu_custom_call" | custom-call | tf_op jit(solution)/shard_map/decode/pallas_call | solution.py:307
Async XLA Ops:
  21.8 21.7 %copy-start = (bf16[128,4,128,128]{3,2,1,0:T(8,128)(2,1)S(1)}, bf16[128,4,128,128]{3,2,1,0:T(8,128)(2,1)}, u32[]{:S(2)}) copy-start(bf16[128,4,128,128]{3,2,1,0:T(8,128)(2,1)} %stiff.3) | copy-start | bytes 50331652
  21.8 21.7 %copy-start.1 = (s32[128,4]{0,1:T(4,128)S(1)}, s32[128,4]{0,1:T(4,128)}, u32[]{:S(2)}) copy-start(s32[128,4]{0,1:T(4,128)} %param.9) | copy-start | bytes 6148
  43.4 26.5 %copy-start.2 = (s32[64,1]{0,1:T(1,128)S(1)}, s32[64,1]{0,1:T(1,128)}, u32[]{:S(2)}) copy-start(s32[64,1]{0,1:T(1,128)} %param.11) | copy-start | bytes 772

commit v8 on v7

--- a/solution.py
+++ b/solution.py
@@ -34,12 +34,24 @@
     return jnp.ceil(8.0 * jnp.log2(jnp.maximum(top, TINY)))
 
 
-def pick_kernel(asked, prolong, stiff, slot, owner, out, heads, held, named, sems):
+def pick_kernel(asked, prolong, stiff, slot, owner, out, heads, blank, clean, held, named, sems):
     load = pltpu.make_async_copy(prolong, held, sems.at[0])
     load.start()
     heads[...] = asked[...].T
     name = pltpu.make_async_copy(heads, named, sems.at[1])
     name.start()
+
+    def clear_sums(a, carry):
+        clean[a] = jnp.zeros(clean.shape[1:], F32)
+        return carry
+
+    lax.fori_loop(0, clean.shape[0], clear_sums, 0, unroll=8)
+
+    def clear_rows(d, carry):
+        blank[d] = jnp.zeros(blank.shape[1:], I16)
+        return carry
+
+    lax.fori_loop(0, blank.shape[0], clear_rows, 0, unroll=8)
     name.wait()
     load.wait()
 
@@ -145,24 +157,12 @@
     )
 
 
-def place_kernel(heads, owner, blocks, out, unit, acc):
+def place_kernel(heads, owner, blocks, blank, clean, out, unit, acc):
     devices, rows, _ = blocks.shape
     aggs = acc.shape[0]
     tiles = acc.shape[2] // LANES
     lanes = lane_ids(8)
     bands = rows // 8
-
-    def clear(a, carry):
-        acc[a] = jnp.zeros(acc.shape[1:], F32)
-        return carry
-
-    lax.fori_loop(0, aggs, clear, 0, unroll=8)
-
-    def clear_out(d, carry):
-        out[d] = jnp.zeros(out.shape[1:], I16)
-        return carry
-
-    lax.fori_loop(0, devices, clear_out, 0, unroll=8)
 
     def add(d, most):
         code = blocks[d].astype(F32)
@@ -181,7 +181,7 @@
             acc[a, :, m * LANES : (m + 1) * LANES] += sums[m] * scale
         return jnp.maximum(most, code[0:8])
 
-    most = lax.fori_loop(0, devices, add, jnp.full((8, LANES), -8.0 * 1024, F32), unroll=32)
+    most = lax.fori_loop(0, devices, add, jnp.full((8, LANES), -8.0 * 1024, F32), unroll=128)
     most = jnp.broadcast_to(most[0:1, SUB + rows : SUB + rows + 1], (8, LANES))
     unit[...] = most
     inverse = jnp.exp2(FLOOR - most * 0.125)[0:1]
@@ -196,7 +196,7 @@
         out[owner[0, a]] = jnp.concatenate(parts, axis=0).astype(I16)
         return carry
 
-    lax.fori_loop(0, aggs, send, 0, unroll=8)
+    lax.fori_loop(0, aggs, send, 0, unroll=64)
 
 
 def decode_kernel(unit, code, out, ready, sems):
@@ -257,20 +257,23 @@
     asking = jnp.concatenate([request[:, None], col_pos, col_pos[:, 0:3]], axis=1)
     asked = swap(asking[:, None, :])[:, 0, :]
 
-    picked, heads = pl.pallas_call(
+    depth = rows * (width // LANES)
+    picked, heads, blank, clean = pl.pallas_call(
         pick_kernel,
         out_shape=(
             jax.ShapeDtypeStruct((devices, rows, dof), BF16),
             jax.ShapeDtypeStruct((8, devices), I32),
+            jax.ShapeDtypeStruct((devices, depth, LANES), I16),
+            jax.ShapeDtypeStruct((aggs, rows, width), F32),
         ),
         in_specs=[vmem, hbm, hbm, hbm, hbm],
-        out_specs=(vmem, vmem),
+        out_specs=(vmem, vmem, vmem, vmem),
         scratch_shapes=[
             pltpu.VMEM((aggs, rows, dof), BF16),
             pltpu.SMEM((8, devices), I32),
             pltpu.SemaphoreType.DMA((2,)),
         ],
-        compiler_params=grant(4),
+        compiler_params=grant(8),
         name="pick",
     )(asked, in_hbm(prolong), in_hbm(stiffness), in_hbm(col_slot.T), in_hbm(coarse_owner.T))
     fetched = swap(picked)
@@ -289,19 +292,19 @@
     )(on_chip(col_slot.T), fetched, on_chip(stiffness))
     blocks = swap(sent)
 
-    depth = rows * (width // LANES)
-    coarse, unit = pl.pallas_call(
+    coarse, unit, _ = pl.pallas_call(
         place_kernel,
         out_shape=(
             jax.ShapeDtypeStruct((devices, depth, LANES), I16),
             jax.ShapeDtypeStruct((8, LANES), F32),
+            jax.ShapeDtypeStruct((aggs, rows, width), F32),
         ),
-        in_specs=[smem, smem, vmem],
-        out_specs=(vmem, vmem),
-        scratch_shapes=[pltpu.VMEM((aggs, rows, width), F32)],
-        compiler_params=grant(16),
+        in_specs=[smem, smem, vmem, vmem, vmem],
+        out_specs=(vmem, vmem, vmem),
+        input_output_aliases={3: 0, 4: 2},
+        compiler_params=grant(8),
         name="place",
-    )(heads, on_chip(coarse_owner.T), blocks)
+    )(heads, on_chip(coarse_owner.T), blocks, blank, clean)
     arrived = swap(coarse)
 
     return pl.pallas_call(

time: 114 us -> 113 us (level)
  no operation moved by 1% of the time
where the time goes in v8:
time: 113 us
  blocking collectives  98.4 us (87%)
  Pallas kernels  13.6 us (12%)
    all_to_all x4, blocking collectives, swap(): return lax.all_to_all(x, AXES, split_axis=0, concat_axis=0, tiled=True)  98.4 us
    pallas_call x1, Pallas kernels, per_device(): pl.pallas_call(partial_kernel, out_shape=jax.ShapeDtypeStruct((devices, r...  6.1 us
    pallas_call x1, Pallas kernels, per_device(): pl.pallas_call(place_kernel, out_shape=(jax.ShapeDtypeStruct((devices, de...  3.58 us
    pallas_call x1, Pallas kernels, per_device(): pl.pallas_call(decode_kernel, out_shape=jax.ShapeDtypeStruct((devices, ro...  2.57 us

profile of v8, /device:TPU:1, one launch (start us, length us, event | category | flops | bytes accessed | tf_op | source)
XLA Modules:
  0.0 112.9 jit_solution(4159250570407458235)
XLA Ops:
  0.0 0.8 pad_add_fusion
  0.8 0.1 copy.12
  0.9 20.9 %all_to_all.20 = s32[128,1,8]{2,1,0:T(1,128)S(1)} all-to-all(s32[128,1,8]{2,1,0:T(1,128)S(1)} %bitcast.11), channel_id=1, replica_groups=mesh['gx'=8,'gy'=16] {'gx','gy'}, dimensions={0} | all-to-all | bytes 8192 | tf_op jit(solution)/shard_map/all_to_all | solution.py:233
  21.8 0.0 copy-start
  21.8 0.0 copy-start.1
  21.8 1.3 %pick.1 = (bf16[128,24,128]{2,1,0:T(8,128)(2,1)S(1)}, s32[8,128]{1,0:T(8,128)S(1)}, s16[128,72,128]{2,1,0:T(8,128)(2,1)S(1)}, f32[64,24,384]{2,1,0:T(8,128)S(1)}) custom-call(s32[128,8]{1,0:T(8,128)S(1)} %bitcast.6, bf16[64,24,128]{2,1,0:T(8,128)(2,1)} %prolong.1, bf16[128,4,128,128]{3,2,1,0:T(8,128)(2,1)} %stiff.3, s32[4,128]{1,0:T(4,128)} %bitcast.7, ...), custom_call_target="tpu_custom_call" | custom-call | tf_op jit(solution)/shard_map/pick/pallas_call | solution.py:261
  23.1 20.3 %all_to_all.21.fetched = bf16[128,24,128]{2,1,0:T(8,128)(2,1)S(1)} all-to-all(bf16[128,24,128]{2,1,0:T(8,128)(2,1)S(1)} %get-tuple-element.12), channel_id=1, replica_groups=mesh['gx'=8,'gy'=16] {'gx','gy'}, dimensions={0} | all-to-all | bytes 1572864 | tf_op jit(solution)/shard_map/all_to_all | solution.py:233
  43.4 0.0 copy-done
  43.4 0.0 copy-done.1
  43.4 0.0 copy-start.2
  43.4 6.1 %partial.1 = s16[128,24,128]{2,1,0:T(8,128)(2,1)S(1)} custom-call(s32[4,128]{1,0:T(4,128)S(1)} %bitcast.8, bf16[128,24,128]{2,1,0:T(8,128)(2,1)S(1)} %all_to_all.21.fetched, bf16[128,4,128,128]{3,2,1,0:T(8,128)(2,1)S(1)} %copy-done), custom_call_target="tpu_custom_call" | custom-call | tf_op jit(solution)/shard_map/partial/pallas_call | solution.py:281
  49.5 20.3 %all_to_all.22.blocks = s16[128,24,128]{2,1,0:T(8,128)(2,1)S(1)} all-to-all(s16[128,24,128]{2,1,0:T(8,128)(2,1)S(1)} %partial.1), channel_id=1, replica_groups=mesh['gx'=8,'gy'=16] {'gx','gy'}, dimensions={0} | all-to-all | bytes 1572864 | tf_op jit(solution)/shard_map/all_to_all | solution.py:233
  69.9 0.0 copy-done.2
  69.9 3.6 %place.1 = (s16[128,72,128]{2,1,0:T(8,128)(2,1)S(1)}, f32[8,128]{1,0:T(8,128)S(1)}, f32[64,24,384]{2,1,0:T(8,128)S(1)}) custom-call(s32[8,128]{1,0:T(8,128)S(1)} %get-tuple-element.11.heads, s32[1,64]{1,0:T(1,128)S(1)} %bitcast.10, s16[128,24,128]{2,1,0:T(8,128)(2,1)S(1)} %all_to_all.22.blocks, ...), custom_call_target="tpu_custom_call", output_to_operand_aliasing={{0}: (3, {}), {2}: (4, {})} | custom-call | tf_op jit(solution)/shard_map/place/pallas_call | solution.py:295
  73.5 36.9 %all_to_all.23.code = s16[128,72,128]{2,1,0:T(8,128)(2,1)S(1)} all-to-all(s16[128,72,128]{2,1,0:T(8,128)(2,1)S(1)} %get-tuple-element.16), channel_id=1, replica_groups=mesh['gx'=8,'gy'=16] {'gx','gy'}, dimensions={0} | all-to-all | bytes 4718592 | tf_op jit(solution)/shard_map/all_to_all | solution.py:233
  110.3 2.6 %decode.1 = f32[128,24,384]{2,1,0:T(8,128)} custom-call(f32[8,128]{1,0:T(8,128)S(1)} %get-tuple-element.15.unit, s16[128,72,128]{2,1,0:T(8,128)(2,1)S(1)} %all_to_all.23.code), custom_call_target="tpu_custom_call" | custom-call | tf_op jit(solution)/shard_map/decode/pallas_call | solution.py:310
Async XLA Ops:
  21.8 21.7 %copy-start = (bf16[128,4,128,128]{3,2,1,0:T(8,128)(2,1)S(1)}, bf16[128,4,128,128]{3,2,1,0:T(8,128)(2,1)}, u32[]{:S(2)}) copy-start(bf16[128,4,128,128]{3,2,1,0:T(8,128)(2,1)} %stiff.3) | copy-start | bytes 50331652
  21.8 21.7 %copy-start.1 = (s32[128,4]{0,1:T(4,128)S(1)}, s32[128,4]{0,1:T(4,128)}, u32[]{:S(2)}) copy-start(s32[128,4]{0,1:T(4,128)} %param.9) | copy-start | bytes 6148
  43.4 26.5 %copy-start.2 = (s32[64,1]{0,1:T(1,128)S(1)}, s32[64,1]{0,1:T(1,128)}, u32[]{:S(2)}) copy-start(s32[64,1]{0,1:T(1,128)} %param.11) | copy-start | bytes 772

commit v9 on v8

--- a/solution.py
+++ b/solution.py
@@ -62,25 +62,29 @@
     lax.fori_loop(0, out.shape[0], step, 0, unroll=16)
 
 
-def partial_kernel(slot, fetched, stiff, out, padded, pairs):
+def partial_kernel(slot, fetched, stiff, out, padded):
     devices, rows, dof = fetched.shape
     per_row = stiff.shape[1]
     lanes = lane_ids(rows)
-    def fill(p, carry):
-        pairs[p] = jnp.zeros(pairs.shape[1:], BF16)
-        for h in range(2):
-            mine = fetched[2 * p + h]
-            padded[2 * p + h, 0:rows, :] = mine
-            padded[2 * p + h, rows:SUB, :] = jnp.zeros((SUB - rows, LANES), BF16)
-            pairs[p, SUB * h : SUB * h + rows, LANES * h : LANES * (h + 1)] = mine
-        return carry
-
-    lax.fori_loop(0, devices // 2, fill, 0, unroll=4)
+    def fill(t, carry):
+        padded[t, 0:rows, :] = fetched[t]
+        padded[t, rows:SUB, :] = jnp.zeros((SUB - rows, LANES), BF16)
+        return carry
+
+    lax.fori_loop(0, devices, fill, 0, unroll=16)
+    none = jnp.zeros((SUB, LANES), BF16)
 
     def products(*accs):
         most = jnp.zeros((rows, 1), F32)
 
         def first(p):
+            left = jnp.concatenate(
+                [
+                    jnp.concatenate([padded[2 * p], none], axis=1),
+                    jnp.concatenate([none, padded[2 * p + 1]], axis=1),
+                ],
+                axis=0,
+            )
             for c in range(2):
                 tile = jnp.concatenate(
                     [
@@ -90,7 +94,7 @@
                     axis=0,
                 )
                 pltpu.matmul_push_rhs(tile, staging_register=c, mxu_index=0)
-                pltpu.matmul_acc_lhs(accs[2 * (p % DEPTH) + c], pairs[p], load_staged_rhs=c)
+                pltpu.matmul_acc_lhs(accs[2 * (p % DEPTH) + c], left, load_staged_rhs=c)
 
         def second(p):
             both = [pltpu.matmul_pop(accs[2 * (p % DEPTH) + c]) for c in range(2)]
@@ -283,10 +287,7 @@
         out_shape=jax.ShapeDtypeStruct((devices, rows, LANES), I16),
         in_specs=[smem, vmem, vmem],
         out_specs=vmem,
-        scratch_shapes=[
-            pltpu.VMEM((devices, SUB, dof), BF16),
-            pltpu.VMEM((devices // 2, 2 * SUB, 2 * dof), BF16),
-        ],
+        scratch_shapes=[pltpu.VMEM((devices, SUB, dof), BF16)],
         compiler_params=grant(16),
         name="partial",
     )(on_chip(col_slot.T), fetched, on_chip(stiffness))

time: 113 us -> 113 us (level)
  no operation moved by 1% of the time
where the time goes in v9:
time: 113 us
  blocking collectives  98.4 us (87%)
  Pallas kernels  13.3 us (12%)
    all_to_all x4, blocking collectives, swap(): return lax.all_to_all(x, AXES, split_axis=0, concat_axis=0, tiled=True)  98.4 us
    pallas_call x1, Pallas kernels, per_device(): pl.pallas_call(partial_kernel, out_shape=jax.ShapeDtypeStruct((devices, r...  5.8 us
    pallas_call x1, Pallas kernels, per_device(): pl.pallas_call(place_kernel, out_shape=(jax.ShapeDtypeStruct((devices, de...  3.58 us
    pallas_call x1, Pallas kernels, per_device(): pl.pallas_call(decode_kernel, out_shape=jax.ShapeDtypeStruct((devices, ro...  2.57 us

profile of v9, /device:TPU:1, one launch (start us, length us, event | category | flops | bytes accessed | tf_op | source)
XLA Modules:
  0.0 112.6 jit_solution(15728932715512940063)
XLA Ops:
  0.0 0.8 pad_add_fusion
  0.8 0.1 copy.12
  0.9 20.9 %all_to_all.20 = s32[128,1,8]{2,1,0:T(1,128)S(1)} all-to-all(s32[128,1,8]{2,1,0:T(1,128)S(1)} %bitcast.11), channel_id=1, replica_groups=mesh['gx'=8,'gy'=16] {'gx','gy'}, dimensions={0} | all-to-all | bytes 8192 | tf_op jit(solution)/shard_map/all_to_all | solution.py:237
  21.8 0.0 copy-start
  21.8 0.0 copy-start.1
  21.8 1.3 %pick.1 = (bf16[128,24,128]{2,1,0:T(8,128)(2,1)S(1)}, s32[8,128]{1,0:T(8,128)S(1)}, s16[128,72,128]{2,1,0:T(8,128)(2,1)S(1)}, f32[64,24,384]{2,1,0:T(8,128)S(1)}) custom-call(s32[128,8]{1,0:T(8,128)S(1)} %bitcast.6, bf16[64,24,128]{2,1,0:T(8,128)(2,1)} %prolong.1, bf16[128,4,128,128]{3,2,1,0:T(8,128)(2,1)} %stiff.3, s32[4,128]{1,0:T(4,128)} %bitcast.7, ...), custom_call_target="tpu_custom_call" | custom-call | tf_op jit(solution)/shard_map/pick/pallas_call | solution.py:265
  23.1 20.3 %all_to_all.21.fetched = bf16[128,24,128]{2,1,0:T(8,128)(2,1)S(1)} all-to-all(bf16[128,24,128]{2,1,0:T(8,128)(2,1)S(1)} %get-tuple-element.12), channel_id=1, replica_groups=mesh['gx'=8,'gy'=16] {'gx','gy'}, dimensions={0} | all-to-all | bytes 1572864 | tf_op jit(solution)/shard_map/all_to_all | solution.py:237
  43.4 0.0 copy-done
  43.4 0.0 copy-done.1
  43.4 0.0 copy-start.2
  43.4 5.8 %partial.1 = s16[128,24,128]{2,1,0:T(8,128)(2,1)S(1)} custom-call(s32[4,128]{1,0:T(4,128)S(1)} %bitcast.8, bf16[128,24,128]{2,1,0:T(8,128)(2,1)S(1)} %all_to_all.21.fetched, bf16[128,4,128,128]{3,2,1,0:T(8,128)(2,1)S(1)} %copy-done), custom_call_target="tpu_custom_call" | custom-call | tf_op jit(solution)/shard_map/partial/pallas_call | solution.py:285
  49.2 20.3 %all_to_all.22.blocks = s16[128,24,128]{2,1,0:T(8,128)(2,1)S(1)} all-to-all(s16[128,24,128]{2,1,0:T(8,128)(2,1)S(1)} %partial.1), channel_id=1, replica_groups=mesh['gx'=8,'gy'=16] {'gx','gy'}, dimensions={0} | all-to-all | bytes 1572864 | tf_op jit(solution)/shard_map/all_to_all | solution.py:237
  69.6 0.0 copy-done.2
  69.6 3.6 %place.1 = (s16[128,72,128]{2,1,0:T(8,128)(2,1)S(1)}, f32[8,128]{1,0:T(8,128)S(1)}, f32[64,24,384]{2,1,0:T(8,128)S(1)}) custom-call(s32[8,128]{1,0:T(8,128)S(1)} %get-tuple-element.11.heads, s32[1,64]{1,0:T(1,128)S(1)} %bitcast.10, s16[128,24,128]{2,1,0:T(8,128)(2,1)S(1)} %all_to_all.22.blocks, ...), custom_call_target="tpu_custom_call", output_to_operand_aliasing={{0}: (3, {}), {2}: (4, {})} | custom-call | tf_op jit(solution)/shard_map/place/pallas_call | solution.py:296
  73.2 36.9 %all_to_all.23.code = s16[128,72,128]{2,1,0:T(8,128)(2,1)S(1)} all-to-all(s16[128,72,128]{2,1,0:T(8,128)(2,1)S(1)} %get-tuple-element.16), channel_id=1, replica_groups=mesh['gx'=8,'gy'=16] {'gx','gy'}, dimensions={0} | all-to-all | bytes 4718592 | tf_op jit(solution)/shard_map/all_to_all | solution.py:237
  110.0 2.6 %decode.1 = f32[128,24,384]{2,1,0:T(8,128)} custom-call(f32[8,128]{1,0:T(8,128)S(1)} %get-tuple-element.15.unit, s16[128,72,128]{2,1,0:T(8,128)(2,1)S(1)} %all_to_all.23.code), custom_call_target="tpu_custom_call" | custom-call | tf_op jit(solution)/shard_map/decode/pallas_call | solution.py:311
Async XLA Ops:
  21.8 21.7 %copy-start = (bf16[128,4,128,128]{3,2,1,0:T(8,128)(2,1)S(1)}, bf16[128,4,128,128]{3,2,1,0:T(8,128)(2,1)}, u32[]{:S(2)}) copy-start(bf16[128,4,128,128]{3,2,1,0:T(8,128)(2,1)} %stiff.3) | copy-start | bytes 50331652
  21.8 21.7 %copy-start.1 = (s32[128,4]{0,1:T(4,128)S(1)}, s32[128,4]{0,1:T(4,128)}, u32[]{:S(2)}) copy-start(s32[128,4]{0,1:T(4,128)} %param.9) | copy-start | bytes 6148
  43.4 26.2 %copy-start.2 = (s32[64,1]{0,1:T(1,128)S(1)}, s32[64,1]{0,1:T(1,128)}, u32[]{:S(2)}) copy-start(s32[64,1]{0,1:T(1,128)} %param.11) | copy-start | bytes 772

commit v10 on v9

--- a/solution.py
+++ b/solution.py
@@ -37,7 +37,8 @@
 def pick_kernel(asked, prolong, stiff, slot, owner, out, heads, blank, clean, held, named, sems):
     load = pltpu.make_async_copy(prolong, held, sems.at[0])
     load.start()
-    heads[...] = asked[...].T
+    heads[0 : asked.shape[1], :] = asked[...].T
+    heads[asked.shape[1] :, :] = jnp.zeros((8 - asked.shape[1], LANES), I32)
     name = pltpu.make_async_copy(heads, named, sems.at[1])
     name.start()
 
@@ -71,7 +72,7 @@
         padded[t, rows:SUB, :] = jnp.zeros((SUB - rows, LANES), BF16)
         return carry
 
-    lax.fori_loop(0, devices, fill, 0, unroll=16)
+    lax.fori_loop(0, devices, fill, 0, unroll=32)
     none = jnp.zeros((SUB, LANES), BF16)
 
     def products(*accs):
@@ -258,7 +259,7 @@
     vmem = pl.BlockSpec(memory_space=pltpu.VMEM)
     hbm = pl.BlockSpec(memory_space=pltpu.HBM)
 
-    asking = jnp.concatenate([request[:, None], col_pos, col_pos[:, 0:3]], axis=1)
+    asking = jnp.concatenate([request[:, None], col_pos], axis=1)
     asked = swap(asking[:, None, :])[:, 0, :]
 
     depth = rows * (width // LANES)

time: 113 us -> 113 us (level)
  no operation moved by 1% of the time
where the time goes in v10:
time: 113 us
  blocking collectives  98.4 us (87%)
  Pallas kernels  13.3 us (12%)
    all_to_all x4, blocking collectives, swap(): return lax.all_to_all(x, AXES, split_axis=0, concat_axis=0, tiled=True)  98.4 us
    pallas_call x1, Pallas kernels, per_device(): pl.pallas_call(partial_kernel, out_shape=jax.ShapeDtypeStruct((devices, r...  5.79 us
    pallas_call x1, Pallas kernels, per_device(): pl.pallas_call(place_kernel, out_shape=(jax.ShapeDtypeStruct((devices, de...  3.58 us
    pallas_call x1, Pallas kernels, per_device(): pl.pallas_call(decode_kernel, out_shape=jax.ShapeDtypeStruct((devices, ro...  2.57 us

profile of v10, /device:TPU:1, one launch (start us, length us, event | category | flops | bytes accessed | tf_op | source)
XLA Modules:
  0.0 112.5 jit_solution(15709948966399576379)
XLA Ops:
  0.0 0.7 pad_add_fusion
  0.7 0.1 copy.11
  0.8 20.9 %all_to_all.20 = s32[128,1,5]{2,1,0:T(1,128)S(1)} all-to-all(s32[128,1,5]{2,1,0:T(1,128)S(1)} %bitcast.10), channel_id=1, replica_groups=mesh['gx'=8,'gy'=16] {'gx','gy'}, dimensions={0} | all-to-all | bytes 5120 | tf_op jit(solution)/shard_map/all_to_all | solution.py:238
  21.7 0.0 copy-start
  21.7 0.0 copy-start.1
  21.7 1.3 %pick.1 = (bf16[128,24,128]{2,1,0:T(8,128)(2,1)S(1)}, s32[8,128]{1,0:T(8,128)S(1)}, s16[128,72,128]{2,1,0:T(8,128)(2,1)S(1)}, f32[64,24,384]{2,1,0:T(8,128)S(1)}) custom-call(s32[128,5]{1,0:T(8,128)S(1)} %bitcast.5, bf16[64,24,128]{2,1,0:T(8,128)(2,1)} %prolong.1, bf16[128,4,128,128]{3,2,1,0:T(8,128)(2,1)} %stiff.3, s32[4,128]{1,0:T(4,128)} %bitcast.6, ...), custom_call_target="tpu_custom_call" | custom-call | tf_op jit(solution)/shard_map/pick/pallas_call | solution.py:266
  23.0 20.3 %all_to_all.21.fetched = bf16[128,24,128]{2,1,0:T(8,128)(2,1)S(1)} all-to-all(bf16[128,24,128]{2,1,0:T(8,128)(2,1)S(1)} %get-tuple-element.12), channel_id=1, replica_groups=mesh['gx'=8,'gy'=16] {'gx','gy'}, dimensions={0} | all-to-all | bytes 1572864 | tf_op jit(solution)/shard_map/all_to_all | solution.py:238
  43.4 0.0 copy-done
  43.4 0.0 copy-done.1
  43.4 0.0 copy-start.2
  43.4 5.8 %partial.1 = s16[128,24,128]{2,1,0:T(8,128)(2,1)S(1)} custom-call(s32[4,128]{1,0:T(4,128)S(1)} %bitcast.7, bf16[128,24,128]{2,1,0:T(8,128)(2,1)S(1)} %all_to_all.21.fetched, bf16[128,4,128,128]{3,2,1,0:T(8,128)(2,1)S(1)} %copy-done), custom_call_target="tpu_custom_call" | custom-call | tf_op jit(solution)/shard_map/partial/pallas_call | solution.py:286
  49.2 20.3 %all_to_all.22.blocks = s16[128,24,128]{2,1,0:T(8,128)(2,1)S(1)} all-to-all(s16[128,24,128]{2,1,0:T(8,128)(2,1)S(1)} %partial.1), channel_id=1, replica_groups=mesh['gx'=8,'gy'=16] {'gx','gy'}, dimensions={0} | all-to-all | bytes 1572864 | tf_op jit(solution)/shard_map/all_to_all | solution.py:238
  69.5 0.0 copy-done.2
  69.5 3.6 %place.1 = (s16[128,72,128]{2,1,0:T(8,128)(2,1)S(1)}, f32[8,128]{1,0:T(8,128)S(1)}, f32[64,24,384]{2,1,0:T(8,128)S(1)}) custom-call(s32[8,128]{1,0:T(8,128)S(1)} %get-tuple-element.11.heads, s32[1,64]{1,0:T(1,128)S(1)} %bitcast.9, s16[128,24,128]{2,1,0:T(8,128)(2,1)S(1)} %all_to_all.22.blocks, ...), custom_call_target="tpu_custom_call", output_to_operand_aliasing={{0}: (3, {}), {2}: (4, {})} | custom-call | tf_op jit(solution)/shard_map/place/pallas_call | solution.py:297
  73.1 36.9 %all_to_all.23.code = s16[128,72,128]{2,1,0:T(8,128)(2,1)S(1)} all-to-all(s16[128,72,128]{2,1,0:T(8,128)(2,1)S(1)} %get-tuple-element.16), channel_id=1, replica_groups=mesh['gx'=8,'gy'=16] {'gx','gy'}, dimensions={0} | all-to-all | bytes 4718592 | tf_op jit(solution)/shard_map/all_to_all | solution.py:238
  110.0 2.6 %decode.1 = f32[128,24,384]{2,1,0:T(8,128)} custom-call(f32[8,128]{1,0:T(8,128)S(1)} %get-tuple-element.15.unit, s16[128,72,128]{2,1,0:T(8,128)(2,1)S(1)} %all_to_all.23.code), custom_call_target="tpu_custom_call" | custom-call | tf_op jit(solution)/shard_map/decode/pallas_call | solution.py:312
Async XLA Ops:
  21.7 21.7 %copy-start = (bf16[128,4,128,128]{3,2,1,0:T(8,128)(2,1)S(1)}, bf16[128,4,128,128]{3,2,1,0:T(8,128)(2,1)}, u32[]{:S(2)}) copy-start(bf16[128,4,128,128]{3,2,1,0:T(8,128)(2,1)} %stiff.3) | copy-start | bytes 50331652
  21.7 21.7 %copy-start.1 = (s32[128,4]{0,1:T(4,128)S(1)}, s32[128,4]{0,1:T(4,128)}, u32[]{:S(2)}) copy-start(s32[128,4]{0,1:T(4,128)} %param.9) | copy-start | bytes 6148
  43.4 26.1 %copy-start.2 = (s32[64,1]{0,1:T(1,128)S(1)}, s32[64,1]{0,1:T(1,128)}, u32[]{:S(2)}) copy-start(s32[64,1]{0,1:T(1,128)} %param.11) | copy-start | bytes 772
